TPU v7x, 256 devices: a whole 4x4x8 slice. The times are simulated.
256 devices in a mesh: dp: 32 (over y, x, core), group: 8 (over z).
Axes of the slice: x: 4, y: 4, z: 8, core: 2. Of those that a mesh axis runs over, the one named last changes fastest.
Arguments:
- patches: bfloat16 [212992, 768], P('dp', 'group'), may hold values from -4 to 4
- embed_weight: bfloat16 [768, 1024], P('dp', 'group'), may hold values from -0.0625 to 0.0625
- channel_gain: float32 [1024], replicated, may hold values from 0.1 to 1.9
- cotangent: bfloat16 [212992, 1024], P('dp', 'group'), may hold values from -6 to 6
Outputs:
- weight_grad: float32 [768, 1024], P('dp', 'group')
- gain_grad: float32 [1024], P('group')
All inputs are finite; a program needn't handle non-finite values.
Results may differ from a plain program's by a relative error of at most 0.00155.
Values may be sent and summed in bfloat16 or wider, within the bound.
No kernel may reach another device: no remote copies, remote signals or barrier semaphores. Data moves between devices by JAX's collectives and lax.ppermute only.
A program may use at most 128 MiB of HBM per device.

v0:
```python
import math

import jax
import jax.numpy as jnp
from jax import lax
from jax.experimental import pallas as pl
from jax.experimental.pallas import tpu as pltpu
from jax.sharding import Mesh
from jax.sharding import PartitionSpec as P

GW = 64
ITERS = 5
DP = ("dp_0", "dp_1", "dp_2")
EPSILON = 1e-05
CHUNKS = (26, 26)
f32, bf16 = jnp.float32, jnp.bfloat16
highest = lax.Precision.HIGHEST
VMEM = pl.BlockSpec(memory_space=pltpu.VMEM)
HBM = pl.BlockSpec(memory_space=pltpu.HBM)


def shifted(value, axis, by):
    size = lax.axis_size(axis)
    return lax.ppermute(value, axis, [(i, (i + by) % size) for i in range(size)])


def gathered_weights(shard):
    count = lax.axis_size(DP)
    copies = jnp.broadcast_to(shard, (count, *shard.shape))
    parts = lax.all_to_all(copies, DP, split_axis=0, concat_axis=0, tiled=True)
    return parts.reshape(-1, shard.shape[1])


def after(value, *others):
    return lax.optimization_barrier((value, *others))


def half_of(block, lower):
    half = block.shape[0] // 2

    def kernel(ref, out):
        out[...] = ref[:half, :] if lower else ref[half:, :]

    return small_call(
        kernel, (jax.ShapeDtypeStruct((half, block.shape[1]), block.dtype),), (block,), "half_of"
    )[0]


def sums_over_ring(chunks, starts, cot, shard):
    weights = gathered_weights(shard).T
    sides = [([c], [c]) for c in chunks]
    for hop in range(3):
        for index, (r, l) in enumerate(sides):
            if hop == 1 and index == 1:
                r[1], weights = after(r[1], weights)
            r.append(shifted(r[-1], "group", 1))
            l.append(shifted(l[-1], "group", -1))
    totals = None
    for (r, l), start in zip(sides, starts):
        far_r = shifted(half_of(r[3], True), "group", 1)
        far_l = shifted(half_of(l[3], False), "group", -1)
        parts = (r[0], r[1], r[2], r[3], l[1], l[2], l[3], far_r, far_l)
        totals = chunk_step(parts, cot, start, weights, totals)
    return totals


TILES = 2


def chunk_kernel(*refs, start, accumulate):
    own, r1, r2, r3, l1, l2, l3, fr, fl, cot, wt = refs[:11]
    rest = refs[11:]
    if accumulate:
        ins, rest = rest[:3], rest[3:]
    ab, hg, sx, big, ce, sems = rest
    width, tokens = own.shape
    half = width // 2
    tile = tokens // TILES
    z = lax.axis_index("group")
    channels = cot.shape[1]
    rows = 8 * width
    blocks = (
        (own, 0, 0),
        (r1, 7, 0),
        (l1, 1, 0),
        (r2, 6, 0),
        (l2, 2, 0),
        (r3, 5, 0),
        (l3, 3, 0),
        (fr, 4, 0),
        (fl, 4, half),
    )

    def copies(step):
        found = []
        for index, (ref, ahead, extra) in enumerate(blocks):
            row = pl.multiple_of(((z + ahead) % 8) * width + extra, 16)
            found.append(
                pltpu.make_async_copy(
                    ref.at[:, step * tile : (step + 1) * tile],
                    big.at[step, pl.ds(row, ref.shape[0]), :],
                    sems.at[step, index],
                )
            )
        found.append(
            pltpu.make_async_copy(
                cot.at[start + step * tile : start + (step + 1) * tile, :],
                ce.at[step, :, :channels],
                sems.at[step, len(blocks)],
            )
        )
        return found

    moves = [copies(step) for step in range(TILES)]
    for step in moves:
        for move in step:
            move.start()
    for step in range(TILES):
        big[step, rows + channels :, :] = jnp.ones((16, tile), bf16)
    for step in range(TILES):
        for move in moves[step]:
            move.wait()
        et = jnp.dot(wt[...], big[step, :rows, :], preferred_element_type=f32)
        big[step, rows : rows + channels, :] = et.astype(bf16)
        ce[step, :, channels:] = et.T.astype(bf16)
        product = jnp.dot(big[step], ce[step], preferred_element_type=f32)
        sums = lax.dot_general(
            jnp.ones((8, tile), bf16),
            big[step, :rows, :],
            (((1,), (1,)), ((), ())),
            preferred_element_type=f32,
        )
        if step or accumulate:
            before = (ab, hg, sx) if step else ins
            ab[...] = before[0][...] + product[:rows]
            hg[...] = before[1][...] + product[rows : rows + channels + 8]
            sx[...] = before[2][...] + sums
        else:
            ab[...] = product[:rows]
            hg[...] = product[rows : rows + channels + 8]
            sx[...] = sums


def chunk_step(parts, cot, start, wt, totals):
    width, tokens = parts[0].shape
    channels = cot.shape[1]
    rows = 8 * width
    outs = (
        jax.ShapeDtypeStruct((rows, 2 * channels), f32),
        jax.ShapeDtypeStruct((channels + 8, 2 * channels), f32),
        jax.ShapeDtypeStruct((8, rows), f32),
    )
    accumulate = totals is not None

    def kernel(*refs):
        chunk_kernel(*refs, start=start, accumulate=accumulate)

    return pl.pallas_call(
        kernel,
        out_shape=outs,
        in_specs=[HBM] * 10 + [VMEM] * (4 if accumulate else 1),
        out_specs=(VMEM, VMEM, VMEM),
        scratch_shapes=[
            pltpu.VMEM((TILES, rows + channels + 16, tokens // TILES), bf16),
            pltpu.VMEM((TILES, tokens // TILES, 2 * channels), bf16),
            pltpu.SemaphoreType.DMA((TILES, 10)),
        ],
        input_output_aliases={11: 0, 12: 1, 13: 2} if accumulate else {},
        cost_estimate=pl.CostEstimate(
            flops=2 * tokens * (rows * 3 * channels + channels * 2 * channels),
            bytes_accessed=2 * tokens * rows,
            transcendentals=0,
        ),
        compiler_params=pltpu.CompilerParams(vmem_limit_bytes=12 * 1024 * 1024),
        name="chunk",
    )(*parts, cot, wt, *(totals or ()))


def small_call(kernel, outs, operands, name):
    return pl.pallas_call(
        kernel,
        out_shape=outs,
        in_specs=[VMEM] * len(operands),
        out_specs=tuple(VMEM for _ in outs),
        cost_estimate=pl.CostEstimate(flops=1_000_000, bytes_accessed=1_000_000, transcendentals=0),
        compiler_params=pltpu.CompilerParams(vmem_limit_bytes=6 * 1024 * 1024),
        name=name,
    )(*operands)


COMMON = 144


def core_stage(totals):
    ab, hg, sx = totals
    share = 24
    channels = ab.shape[1] // 2

    def kernel(ab, hg, sx, keep, send):
        core = lax.axis_index("dp_2")
        for ref, parity in ((keep, core), (send, 1 - core)):
            for block in range(16):
                row = pl.multiple_of(block * 2 * share + parity * share, 8)
                for side in range(2):
                    to = (block * 2 + side) * share
                    ref[to : to + share, :] = ab[
                        pl.ds(row, share), side * channels : (side + 1) * channels
                    ]
            low = lax.broadcasted_iota(jnp.int32, (GW, channels), 1) < GW
            base = 32 * share
            for side in range(2):
                cols = slice(side * channels, (side + 1) * channels)
                ref[base + side * GW : base + (side + 1) * GW, :] = jnp.where(
                    low, hg[:GW, cols], hg[GW : 2 * GW, cols]
                )
            base += 2 * GW
            ref[base : base + COMMON - 2 * GW, :] = jnp.zeros((COMMON - 2 * GW, channels), f32)
            for side in range(2):
                ref[base + side : base + side + 1, :] = hg[
                    2 * GW : 2 * GW + 1, side * channels : (side + 1) * channels
                ]
            for part in range(6):
                ref[base + 8 + part : base + 9 + part, :] = sx[
                    0:1, part * channels : (part + 1) * channels
                ]

    shape = jax.ShapeDtypeStruct((32 * share + COMMON, channels), f32)
    return small_call(kernel, (shape, shape), (ab, hg, sx), "core_stage")


def axis_stage(axis, received, rows_out):
    rows_in, channels = received[0].shape

    def kernel(*refs):
        ins, outs = refs[: len(received)], refs[len(received) :]
        here = lax.axis_index(axis)
        shared = ins[0][rows_in - COMMON :, :]
        for ref in ins[1:]:
            shared = shared + ref[rows_in - COMMON :, :]
        for step, out in enumerate(outs):
            row = pl.multiple_of(((here + step) % 4) * rows_out, 8)
            block = ins[0][pl.ds(row, rows_out), :]
            for ref in ins[1:]:
                block = block + ref[pl.ds(row, rows_out), :]
            out[:rows_out, :] = block
            out[rows_out:, :] = shared

    shape = jax.ShapeDtypeStruct((rows_out + COMMON, channels), f32)
    return small_call(kernel, (shape,) * 4, received, "axis_stage")


def dot(left, right):
    return jnp.dot(left, right, preferred_element_type=f32, precision=highest)


def last_stage(received, gain, total_tokens):
    channels = received[0].shape[1]
    share = 24
    loss_scale = 1.0 / math.sqrt(total_tokens)
    inverse = 1.0 / total_tokens

    def kernel(*refs):
        ins, gain_ref = refs[: len(received)], refs[len(received)]
        weight_out, gain_out = refs[len(received) + 1 :]
        everything = ins[0][...]
        for ref in ins[1:]:
            everything = everything + ref[...]
        a_rows = everything[:share]
        b_rows = everything[share : 2 * share]
        base = 2 * share
        lane = lax.broadcasted_iota(jnp.int32, (channels, channels), 1)
        row = lax.broadcasted_iota(jnp.int32, (channels, channels), 0)
        same = (lane < GW) == (row < GW)
        eye = (lane == row).astype(f32)
        lane1 = lax.broadcasted_iota(jnp.int32, (1, channels), 1)

        def blocks(flat):
            return jnp.where(same, jnp.concatenate([flat, flat], axis=0), 0.0)

        def per_group(line):
            low = jnp.sum(jnp.where(lane1 < GW, line, 0.0), axis=1, keepdims=True)
            high = jnp.sum(jnp.where(lane1 < GW, 0.0, line), axis=1, keepdims=True)
            return jnp.where(lane1 < GW, low, high)

        def column(line):
            return jnp.sum(eye * line, axis=1, keepdims=True)

        h_t = blocks(everything[base : base + GW])
        gram = blocks(everything[base + GW : base + 2 * GW])
        base += 2 * GW
        cot_sum = everything[base : base + 1]
        mean = everything[base + 1 : base + 2] * inverse
        patch_sums = everything[base + 8 : base + 14]
        mean_col = column(mean)
        covariance = gram * inverse - jnp.where(same, mean_col * mean, 0.0) + EPSILON * eye
        h_t = h_t - jnp.where(same, mean_col * cot_sum, 0.0)
        scaled_gain = gain_ref[pl.ds(lax.axis_index("group"), 1), :] * loss_scale
        q_t = h_t * scaled_gain
        toward = 0.5 * (q_t + q_t.T)
        trace = per_group(jnp.sum(covariance * eye, axis=0, keepdims=True))
        normed = covariance / trace
        power = 1.5 * eye - 0.5 * normed
        change = -0.5 * toward
        right = jnp.concatenate([normed, toward], axis=1)
        for _ in range(ITERS - 1):
            both = jnp.concatenate([power, change], axis=0)
            first = dot(both, power)
            second = dot(both, right)
            square, mixed = first[:channels], first[channels:]
            times = second[:channels, :channels]
            times_change = second[channels:, :channels] + second[:channels, channels:]
            square_change = mixed + mixed.T
            third = dot(square, jnp.concatenate([times, times_change], axis=1))
            fourth = dot(square_change, times)
            power, change = (
                1.5 * power - 0.5 * third[:, :channels],
                1.5 * change - 0.5 * (third[:, channels:] + fourth),
            )
        root = lax.rsqrt(trace)
        whitener = power * root
        spread = per_group(jnp.sum(change * covariance, axis=0, keepdims=True))
        scale_part = per_group(jnp.sum(toward * power, axis=0, keepdims=True))
        cubed = root * root * root
        grad_cov = cubed * change - eye * (cubed * root * root * spread + 0.5 * cubed * scale_part)
        symmetric = grad_cov * (2.0 * inverse)
        gain_out[...] = jnp.sum(whitener * h_t, axis=0, keepdims=True) * loss_scale
        device = lax.axis_index(DP)
        lanes = lax.broadcasted_iota(jnp.int32, (share, channels), 1)
        rows = lax.broadcasted_iota(jnp.int32, (share, channels), 0) + device * share
        picked = jnp.zeros((share, channels), f32)
        for part in range(6):
            picked = picked + jnp.where(
                lanes + part * channels == rows, patch_sums[part : part + 1], 0.0
            )
        patch_sum = jnp.sum(picked, axis=1, keepdims=True)
        a_rows = (a_rows - patch_sum * (cot_sum * inverse)) * scaled_gain
        b_rows = b_rows - patch_sum * mean
        weight_out[...] = dot(a_rows, whitener) + dot(b_rows, symmetric)

    outs = (
        jax.ShapeDtypeStruct((share, channels), f32),
        jax.ShapeDtypeStruct((1, channels), f32),
    )
    return small_call(kernel, outs, (*received, gain), "last_stage")


def body(patches, embed_weight, channel_gain, cotangent):
    tok_rows = patches.shape[0]
    total_tokens = tok_rows * lax.axis_size(DP)
    unit = tok_rows // sum(CHUNKS)
    bounds = [unit * sum(CHUNKS[:i]) for i in range(len(CHUNKS) + 1)]
    flipped = patches.T
    totals = sums_over_ring(
        [flipped[:, lo:hi] for lo, hi in zip(bounds, bounds[1:])], bounds, cotangent, embed_weight
    )
    keep, send = core_stage(totals)
    keep, *send = axis_stage("dp_0", (keep, shifted(send, "dp_2", 1)), 192)
    came = [shifted(s, "dp_0", i + 1) for i, s in enumerate(send)]
    keep, *send = axis_stage("dp_1", (keep, *came), 48)
    came = [shifted(s, "dp_1", i + 1) for i, s in enumerate(send)]
    gain = channel_gain.reshape(-1, embed_weight.shape[1])
    weight_grad, gain_grad = last_stage((keep, *came), gain, total_tokens)
    return weight_grad, gain_grad.reshape(-1)


def solution(mesh):
    torus = Mesh(
        mesh.devices.reshape(4, 4, 2, mesh.shape["group"]), ("dp_0", "dp_1", "dp_2", "group")
    )
    return jax.shard_map(
        body,
        mesh=torus,
        in_specs=(P(DP, "group"), P(DP, "group"), P(), P(DP, "group")),
        out_specs=(P(DP, "group"), P("group")),
        check_vma=False,
    )
```

profile of v0, /device:TPU:6, one launch (start us, length us, event | category | flops | bytes accessed | tf_op | source)
XLA Modules:
  0.0 138.5 jit_solution(9681940127287163205)
XLA Ops:
  0.6 1.4 fusion
  2.0 2.0 %collective-permute-start.8 = (bf16[96,3328]{1,0:T(8,128)(2,1)S(1)}, bf16[96,3328]{1,0:T(8,128)(2,1)S(1)}, u32[]{:S(2)}, u32[]{:S(2)}) collective-permute-start(bf16[96,3328]{1,0:T(8,128)(2,1)S(1)} %get-tuple-element.42.refs_0_), channel_id=1, source_target_pairs={{0,1},{1,2},{2,3},{3,4},{4,5},{5,6},{6,7},{7,0},{8,9},{9,10},{10,1... | collective-permute-start | bytes 1916936 | tf_op jit(solution)/shard_map/ppermute | solution.py:24
  4.0 4.0 %collective-permute-start.11 = (bf16[96,3328]{1,0:T(8,128)(2,1)S(1)}, bf16[96,3328]{1,0:T(8,128)(2,1)}, u32[]{:S(2)}, u32[]{:S(2)}) collective-permute-start(bf16[96,3328]{1,0:T(8,128)(2,1)S(1)} %get-tuple-element.42.refs_0_), channel_id=1, source_target_pairs={{0,7},{1,0},{2,1},{3,2},{4,3},{5,4},{6,5},{7,6},{8,15},{9,8},{10,9... | collective-permute-start | bytes 1916936 | tf_op jit(solution)/shard_map/ppermute | solution.py:24
  8.0 0.0 collective-permute-start
  8.0 3.2 %collective-permute-start.3 = (bf16[96,3328]{1,0:T(8,128)(2,1)S(1)}, bf16[96,3328]{1,0:T(8,128)(2,1)S(1)}, u32[]{:S(2)}, u32[]{:S(2)}) collective-permute-start(bf16[96,3328]{1,0:T(8,128)(2,1)S(1)} %get-tuple-element.43.refs_0_), channel_id=1, source_target_pairs={{0,7},{1,0},{2,1},{3,2},{4,3},{5,4},{6,5},{7,6},{8,15},{9,8},{10,9... | collective-permute-start | bytes 1916936 | tf_op jit(solution)/shard_map/ppermute | solution.py:24
  11.3 11.9 %collective-permute-done.8.refs_1_ = bf16[96,3328]{1,0:T(8,128)(2,1)S(1)} collective-permute-done((bf16[96,3328]{1,0:T(8,128)(2,1)S(1)}, bf16[96,3328]{1,0:T(8,128)(2,1)S(1)}, u32[]{:S(2)}, u32[]{:S(2)}) %collective-permute-start.8) | collective-permute-done | bytes 639008 | tf_op jit(solution)/shard_map/ppermute | solution.py:24
  23.2 0.0 collective-permute-start.9
  23.2 0.0 collective-permute-done.11.refs_4_
  23.2 3.4 %collective-permute-start.12 = (bf16[96,3328]{1,0:T(8,128)(2,1)}, bf16[96,3328]{1,0:T(8,128)(2,1)}, u32[]{:S(2)}, u32[]{:S(2)}) collective-permute-start(bf16[96,3328]{1,0:T(8,128)(2,1)} %collective-permute-done.11.refs_4_), channel_id=1, source_target_pairs={{0,7},{1,0},{2,1},{3,2},{4,3},{5,4},{6,5},{7,6},{8,15},{9,8},{10,9... | collective-permute-start | bytes 1916936 | tf_op jit(solution)/shard_map/ppermute | solution.py:24
  26.6 14.0 %all_to_all.5 = bf16[32,24,128]{2,1,0:T(8,128)(2,1)} all-to-all(bf16[32,24,128]{2,1,0:T(8,128)(2,1)S(1)} %broadcast_in_dim.3), channel_id=1, replica_groups=mesh['dp_0'=4,'dp_1'=4,'dp_2'=2,'group'=8] {'dp_0','dp_1','dp_2'}, dimensions={0} | all-to-all | bytes 393216 | tf_op jit(solution)/shard_map/all_to_all | solution.py:30
  40.7 1.1 copy.10
  41.7 0.0 collective-permute-done.refs_1_
  41.8 0.1 collective-permute-start.1
  41.8 0.0 collective-permute-done.3.refs_4_
  41.9 3.2 %collective-permute-start.4 = (bf16[96,3328]{1,0:T(8,128)(2,1)S(1)}, bf16[96,3328]{1,0:T(8,128)(2,1)S(1)}, u32[]{:S(2)}, u32[]{:S(2)}) collective-permute-start(bf16[96,3328]{1,0:T(8,128)(2,1)S(1)} %collective-permute-done.3.refs_4_), channel_id=1, source_target_pairs={{0,7},{1,0},{2,1},{3,2},{4,3},{5,4},{6,5},{7,6},{8,15},{9,8},{10,9... | collective-permute-start | bytes 1916936 | tf_op jit(solution)/shard_map/ppermute | solution.py:24
  45.1 5.6 %collective-permute-done.9.refs_2_ = bf16[96,3328]{1,0:T(8,128)(2,1)} collective-permute-done((bf16[96,3328]{1,0:T(8,128)(2,1)S(1)}, bf16[96,3328]{1,0:T(8,128)(2,1)}, u32[]{:S(2)}, u32[]{:S(2)}) %collective-permute-start.9) | collective-permute-done | bytes 639008 | tf_op jit(solution)/shard_map/ppermute | solution.py:24
  50.7 0.0 collective-permute-start.10
  50.7 3.3 %collective-permute-start.13 = (bf16[96,3328]{1,0:T(8,128)(2,1)}, bf16[96,3328]{1,0:T(8,128)(2,1)S(1)}, u32[]{:S(2)}, u32[]{:S(2)}) collective-permute-start(bf16[96,3328]{1,0:T(8,128)(2,1)} %collective-permute-done.12.refs_5_), channel_id=1, source_target_pairs={{0,7},{1,0},{2,1},{3,2},{4,3},{5,4},{6,5},{7,6},{8,15},{9,8},{10,9... | collective-permute-start | bytes 1916936 | tf_op jit(solution)/shard_map/ppermute | solution.py:24
  54.0 10.3 %collective-permute-done.1.refs_2_ = bf16[96,3328]{1,0:T(8,128)(2,1)S(1)} collective-permute-done((bf16[96,3328]{1,0:T(8,128)(2,1)S(1)}, bf16[96,3328]{1,0:T(8,128)(2,1)S(1)}, u32[]{:S(2)}, u32[]{:S(2)}) %collective-permute-start.1) | collective-permute-done | bytes 639008 | tf_op jit(solution)/shard_map/ppermute | solution.py:24
  64.3 3.3 %collective-permute-start.5 = (bf16[96,3328]{1,0:T(8,128)(2,1)S(1)}, bf16[96,3328]{1,0:T(8,128)(2,1)S(1)}, u32[]{:S(2)}, u32[]{:S(2)}) collective-permute-start(bf16[96,3328]{1,0:T(8,128)(2,1)S(1)} %collective-permute-done.4.refs_5_), channel_id=1, source_target_pairs={{0,7},{1,0},{2,1},{3,2},{4,3},{5,4},{6,5},{7,6},{8,15},{9,8},{10,9... | collective-permute-start | bytes 1916936 | tf_op jit(solution)/shard_map/ppermute | solution.py:24
  67.6 10.4 %collective-permute-done.10.ref.refs_3_ = bf16[96,3328]{1,0:T(8,128)(2,1)S(1)} collective-permute-done((bf16[96,3328]{1,0:T(8,128)(2,1)}, bf16[96,3328]{1,0:T(8,128)(2,1)S(1)}, u32[]{:S(2)}, u32[]{:S(2)}) %collective-permute-start.10) | collective-permute-done | bytes 639008 | tf_op jit(solution)/shard_map/ppermute | solution.py:24
  78.0 0.0 copy-start.1
  78.0 0.1 collective-permute-start.14
  78.1 3.3 %collective-permute-start.15 = (bf16[48,3328]{1,0:T(8,128)(2,1)S(1)}, bf16[48,3328]{1,0:T(8,128)(2,1)S(1)}, u32[]{:S(2)}, u32[]{:S(2)}) collective-permute-start(bf16[48,3328]{1,0:T(8,128)(2,1)S(1)} %half_of.7), channel_id=1, source_target_pairs={{0,7},{1,0},{2,1},{3,2},{4,3},{5,4},{6,5},{7,6},{8,15},{9,8},{10,9... | collective-permute-start | bytes 958472 | tf_op jit(solution)/shard_map/ppermute | solution.py:24
  81.4 10.2 %collective-permute-done.2.ref.refs_3_ = bf16[96,3328]{1,0:T(8,128)(2,1)S(1)} collective-permute-done((bf16[96,3328]{1,0:T(8,128)(2,1)S(1)}, bf16[96,3328]{1,0:T(8,128)(2,1)S(1)}, u32[]{:S(2)}, u32[]{:S(2)}) %collective-permute-start.2) | collective-permute-done | bytes 639008 | tf_op jit(solution)/shard_map/ppermute | solution.py:24
  91.7 0.3 collective-permute-start.6
  92.0 3.3 %collective-permute-start.7 = (bf16[48,3328]{1,0:T(8,128)(2,1)S(1)}, bf16[48,3328]{1,0:T(8,128)(2,1)S(1)}, u32[]{:S(2)}, u32[]{:S(2)}) collective-permute-start(bf16[48,3328]{1,0:T(8,128)(2,1)S(1)} %half_of.5), channel_id=1, source_target_pairs={{0,7},{1,0},{2,1},{3,2},{4,3},{5,4},{6,5},{7,6},{8,15},{9,8},{10,9... | collective-permute-start | bytes 958472 | tf_op jit(solution)/shard_map/ppermute | solution.py:24
  95.3 3.2 %collective-permute-done.14.refs_7_ = bf16[48,3328]{1,0:T(8,128)(2,1)S(1)} collective-permute-done((bf16[48,3328]{1,0:T(8,128)(2,1)S(1)}, bf16[48,3328]{1,0:T(8,128)(2,1)S(1)}, u32[]{:S(2)}, u32[]{:S(2)}) %collective-permute-start.14) | collective-permute-done | bytes 319520 | tf_op jit(solution)/shard_map/ppermute | solution.py:24
  98.5 5.9 %chunk.2 = (f32[768,256]{1,0:T(8,128)S(1)}, f32[136,256]{1,0:T(8,128)S(1)}, f32[8,768]{1,0:T(8,128)S(1)}) custom-call(bf16[96,3328]{1,0:T(8,128)(2,1)S(1)} %get-tuple-element.42.refs_0_, bf16[96,3328]{1,0:T(8,128)(2,1)S(1)} %collective-permute-done.8.refs_1_, bf16[96,3328]{1,0:T(8,128)(2,1)} %collective-permute-done.9.refs_2_, ...), custom_call_target="tpu_custom_call" | custom-call | flops 2181038080 | bytes 5111808 | tf_op jit(solution)/shard_map/chunk/pallas_call | solution.py:158
  104.4 0.1 collective-permute-done.6.refs_7_
  104.5 5.5 %chunk.3 = (f32[768,256]{1,0:T(8,128)S(1)}, f32[136,256]{1,0:T(8,128)S(1)}, f32[8,768]{1,0:T(8,128)S(1)}) custom-call(bf16[96,3328]{1,0:T(8,128)(2,1)S(1)} %get-tuple-element.43.refs_0_, bf16[96,3328]{1,0:T(8,128)(2,1)S(1)} %collective-permute-done.refs_1_, ...), custom_call_target="tpu_custom_call", output_to_operand_aliasing={{0}: (11, {}), {1}: (12, {}), {2}: (13, {})} | custom-call | flops 2181038080 | bytes 5111808 | tf_op jit(solution)/shard_map/chunk/pallas_call | solution.py:158
  110.0 0.0 copy-start
  110.0 0.1 core_stage.1
  110.1 0.1 collective-permute-start.16
  110.2 1.8 %collective-permute-done.16.refs_1_ = f32[912,128]{1,0:T(8,128)S(1)} collective-permute-done((f32[912,128]{1,0:T(8,128)S(1)}, f32[912,128]{1,0:T(8,128)S(1)}, u32[]{:S(2)}, u32[]{:S(2)}) %collective-permute-start.16) | collective-permute-done | bytes 466976 | tf_op jit(solution)/shard_map/ppermute | solution.py:24
  112.0 0.1 axis_stage.2
  112.1 1.7 %collective-permute-start.17 = (f32[336,128]{1,0:T(8,128)S(1)}, f32[336,128]{1,0:T(8,128)S(1)}, u32[]{:S(2)}, u32[]{:S(2)}) collective-permute-start(f32[336,128]{1,0:T(8,128)S(1)} %get-tuple-element.33), channel_id=1, source_target_pairs={{0,64},{64,128},{128,192},{192,0},{1,65},{65,129},{129,193},{193,1... | collective-permute-start | bytes 516104 | tf_op jit(solution)/shard_map/ppermute | solution.py:24
  113.8 2.9 %collective-permute-start.18 = (f32[336,128]{1,0:T(8,128)S(1)}, f32[336,128]{1,0:T(8,128)S(1)}, u32[]{:S(2)}, u32[]{:S(2)}) collective-permute-start(f32[336,128]{1,0:T(8,128)S(1)} %get-tuple-element.34), channel_id=1, source_target_pairs={{0,128},{64,192},{128,0},{192,64},{1,129},{65,193},{129,1},{193,65... | collective-permute-start | bytes 516104 | tf_op jit(solution)/shard_map/ppermute | solution.py:24
  116.7 1.3 collective-permute-start.19
  118.0 1.9 %collective-permute-done.17.refs_1_ = f32[336,128]{1,0:T(8,128)S(1)} collective-permute-done((f32[336,128]{1,0:T(8,128)S(1)}, f32[336,128]{1,0:T(8,128)S(1)}, u32[]{:S(2)}, u32[]{:S(2)}) %collective-permute-start.17) | collective-permute-done | bytes 172064 | tf_op jit(solution)/shard_map/ppermute | solution.py:24
  119.9 4.9 %collective-permute-done.18.refs_2_ = f32[336,128]{1,0:T(8,128)S(1)} collective-permute-done((f32[336,128]{1,0:T(8,128)S(1)}, f32[336,128]{1,0:T(8,128)S(1)}, u32[]{:S(2)}, u32[]{:S(2)}) %collective-permute-start.18) | collective-permute-done | bytes 172064 | tf_op jit(solution)/shard_map/ppermute | solution.py:24
  124.8 0.6 collective-permute-start.20
  125.3 2.4 %collective-permute-start.21 = (f32[192,128]{1,0:T(8,128)S(1)}, f32[192,128]{1,0:T(8,128)S(1)}, u32[]{:S(2)}, u32[]{:S(2)}) collective-permute-start(f32[192,128]{1,0:T(8,128)S(1)} %get-tuple-element.38), channel_id=1, source_target_pairs={{0,32},{16,48},{32,0},{48,16},{1,33},{17,49},{33,1},{49,17},{2,34}... | collective-permute-start | bytes 294920 | tf_op jit(solution)/shard_map/ppermute | solution.py:24
  127.8 0.0 collective-permute-start.22
  127.8 2.1 %collective-permute-done.20.refs_1_ = f32[192,128]{1,0:T(8,128)S(1)} collective-permute-done((f32[192,128]{1,0:T(8,128)S(1)}, f32[192,128]{1,0:T(8,128)S(1)}, u32[]{:S(2)}, u32[]{:S(2)}) %collective-permute-start.20) | collective-permute-done | bytes 98336 | tf_op jit(solution)/shard_map/ppermute | solution.py:24
  129.9 2.5 %collective-permute-done.21.refs_2_ = f32[192,128]{1,0:T(8,128)S(1)} collective-permute-done((f32[192,128]{1,0:T(8,128)S(1)}, f32[192,128]{1,0:T(8,128)S(1)}, u32[]{:S(2)}, u32[]{:S(2)}) %collective-permute-start.21) | collective-permute-done | bytes 98336 | tf_op jit(solution)/shard_map/ppermute | solution.py:24
  132.4 1.2 collective-permute-done.22.refs_3_
  133.6 4.9 %last_stage.1 = (f32[24,128]{1,0:T(8,128)}, f32[1,128]{1,0:T(1,128)}) custom-call(f32[192,128]{1,0:T(8,128)S(1)} %get-tuple-element.36.refs_0_, f32[192,128]{1,0:T(8,128)S(1)} %collective-permute-done.20.refs_1_, f32[192,128]{1,0:T(8,128)S(1)} %collective-permute-done.21.refs_2_, f32[192,128]{1,0:T(8,128)S(1)} %collective-permute-done.22.refs_3_, ...), custom_call_target="tpu_custom_call" | custom-call | flops 1000000 | bytes 1000000 | tf_op jit(solution)/shard_map/last_stage/pallas_call | solution.py:180
  (18 shorter events, 0.2 us)
Async XLA Ops:
  0.6 26.0 %copy-start.2 = (bf16[24,128]{1,0:T(8,128)(2,1)S(1)}, bf16[24,128]{1,0:T(8,128)(2,1)}, u32[]{:S(2)}) copy-start(bf16[24,128]{1,0:T(8,128)(2,1)} %param.5) | copy-start | bytes 18436
  2.0 21.2 %collective-permute-start.8 = (bf16[96,3328]{1,0:T(8,128)(2,1)S(1)}, bf16[96,3328]{1,0:T(8,128)(2,1)S(1)}, u32[]{:S(2)}, u32[]{:S(2)}) collective-permute-start(bf16[96,3328]{1,0:T(8,128)(2,1)S(1)} %get-tuple-element.42.refs_0_), channel_id=1, source_target_pairs={{0,1},{1,2},{2,3},{3,4},{4,5},{5,6},{6,7},{7,0},{8,9},{9,10},{10,1... | collective-permute-start | bytes 1916936 | tf_op jit(solution)/shard_map/ppermute | solution.py:24
  4.0 19.2 %collective-permute-start.11 = (bf16[96,3328]{1,0:T(8,128)(2,1)S(1)}, bf16[96,3328]{1,0:T(8,128)(2,1)}, u32[]{:S(2)}, u32[]{:S(2)}) collective-permute-start(bf16[96,3328]{1,0:T(8,128)(2,1)S(1)} %get-tuple-element.42.refs_0_), channel_id=1, source_target_pairs={{0,7},{1,0},{2,1},{3,2},{4,3},{5,4},{6,5},{7,6},{8,15},{9,8},{10,9... | collective-permute-start | bytes 1916936 | tf_op jit(solution)/shard_map/ppermute | solution.py:24
  8.0 33.7 %collective-permute-start = (bf16[96,3328]{1,0:T(8,128)(2,1)S(1)}, bf16[96,3328]{1,0:T(8,128)(2,1)S(1)}, u32[]{:S(2)}, u32[]{:S(2)}) collective-permute-start(bf16[96,3328]{1,0:T(8,128)(2,1)S(1)} %get-tuple-element.43.refs_0_), channel_id=1, source_target_pairs={{0,1},{1,2},{2,3},{3,4},{4,5},{5,6},{6,7},{7,0},{8,9},{9,10},{10,1... | collective-permute-start | bytes 1916936 | tf_op jit(solution)/shard_map/ppermute | solution.py:24
  8.0 33.8 %collective-permute-start.3 = (bf16[96,3328]{1,0:T(8,128)(2,1)S(1)}, bf16[96,3328]{1,0:T(8,128)(2,1)S(1)}, u32[]{:S(2)}, u32[]{:S(2)}) collective-permute-start(bf16[96,3328]{1,0:T(8,128)(2,1)S(1)} %get-tuple-element.43.refs_0_), channel_id=1, source_target_pairs={{0,7},{1,0},{2,1},{3,2},{4,3},{5,4},{6,5},{7,6},{8,15},{9,8},{10,9... | collective-permute-start | bytes 1916936 | tf_op jit(solution)/shard_map/ppermute | solution.py:24
  23.2 27.5 %collective-permute-start.9 = (bf16[96,3328]{1,0:T(8,128)(2,1)S(1)}, bf16[96,3328]{1,0:T(8,128)(2,1)}, u32[]{:S(2)}, u32[]{:S(2)}) collective-permute-start(bf16[96,3328]{1,0:T(8,128)(2,1)S(1)} %collective-permute-done.8.refs_1_), channel_id=1, source_target_pairs={{0,1},{1,2},{2,3},{3,4},{4,5},{5,6},{6,7},{7,0},{8,9},{9,10},{10,1... | collective-permute-start | bytes 1916936 | tf_op jit(solution)/shard_map/ppermute | solution.py:24
  23.2 27.5 %collective-permute-start.12 = (bf16[96,3328]{1,0:T(8,128)(2,1)}, bf16[96,3328]{1,0:T(8,128)(2,1)}, u32[]{:S(2)}, u32[]{:S(2)}) collective-permute-start(bf16[96,3328]{1,0:T(8,128)(2,1)} %collective-permute-done.11.refs_4_), channel_id=1, source_target_pairs={{0,7},{1,0},{2,1},{3,2},{4,3},{5,4},{6,5},{7,6},{8,15},{9,8},{10,9... | collective-permute-start | bytes 1916936 | tf_op jit(solution)/shard_map/ppermute | solution.py:24
  41.8 22.5 %collective-permute-start.1 = (bf16[96,3328]{1,0:T(8,128)(2,1)S(1)}, bf16[96,3328]{1,0:T(8,128)(2,1)S(1)}, u32[]{:S(2)}, u32[]{:S(2)}) collective-permute-start(bf16[96,3328]{1,0:T(8,128)(2,1)S(1)} %collective-permute-done.refs_1_), channel_id=1, source_target_pairs={{0,1},{1,2},{2,3},{3,4},{4,5},{5,6},{6,7},{7,0},{8,9},{9,10},{10,1... | collective-permute-start | bytes 1916936 | tf_op jit(solution)/shard_map/ppermute | solution.py:24
  41.9 22.4 %collective-permute-start.4 = (bf16[96,3328]{1,0:T(8,128)(2,1)S(1)}, bf16[96,3328]{1,0:T(8,128)(2,1)S(1)}, u32[]{:S(2)}, u32[]{:S(2)}) collective-permute-start(bf16[96,3328]{1,0:T(8,128)(2,1)S(1)} %collective-permute-done.3.refs_4_), channel_id=1, source_target_pairs={{0,7},{1,0},{2,1},{3,2},{4,3},{5,4},{6,5},{7,6},{8,15},{9,8},{10,9... | collective-permute-start | bytes 1916936 | tf_op jit(solution)/shard_map/ppermute | solution.py:24
  50.7 27.3 %collective-permute-start.10 = (bf16[96,3328]{1,0:T(8,128)(2,1)}, bf16[96,3328]{1,0:T(8,128)(2,1)S(1)}, u32[]{:S(2)}, u32[]{:S(2)}) collective-permute-start(bf16[96,3328]{1,0:T(8,128)(2,1)} %collective-permute-done.9.refs_2_), channel_id=1, source_target_pairs={{0,1},{1,2},{2,3},{3,4},{4,5},{5,6},{6,7},{7,0},{8,9},{9,10},{10,1... | collective-permute-start | bytes 1916936 | tf_op jit(solution)/shard_map/ppermute | solution.py:24
  50.7 27.4 %collective-permute-start.13 = (bf16[96,3328]{1,0:T(8,128)(2,1)}, bf16[96,3328]{1,0:T(8,128)(2,1)S(1)}, u32[]{:S(2)}, u32[]{:S(2)}) collective-permute-start(bf16[96,3328]{1,0:T(8,128)(2,1)} %collective-permute-done.12.refs_5_), channel_id=1, source_target_pairs={{0,7},{1,0},{2,1},{3,2},{4,3},{5,4},{6,5},{7,6},{8,15},{9,8},{10,9... | collective-permute-start | bytes 1916936 | tf_op jit(solution)/shard_map/ppermute | solution.py:24
  64.2 27.4 %collective-permute-start.2 = (bf16[96,3328]{1,0:T(8,128)(2,1)S(1)}, bf16[96,3328]{1,0:T(8,128)(2,1)S(1)}, u32[]{:S(2)}, u32[]{:S(2)}) collective-permute-start(bf16[96,3328]{1,0:T(8,128)(2,1)S(1)} %collective-permute-done.1.refs_2_), channel_id=1, source_target_pairs={{0,1},{1,2},{2,3},{3,4},{4,5},{5,6},{6,7},{7,0},{8,9},{9,10},{10,1... | collective-permute-start | bytes 1916936 | tf_op jit(solution)/shard_map/ppermute | solution.py:24
  64.3 27.7 %collective-permute-start.5 = (bf16[96,3328]{1,0:T(8,128)(2,1)S(1)}, bf16[96,3328]{1,0:T(8,128)(2,1)S(1)}, u32[]{:S(2)}, u32[]{:S(2)}) collective-permute-start(bf16[96,3328]{1,0:T(8,128)(2,1)S(1)} %collective-permute-done.4.refs_5_), channel_id=1, source_target_pairs={{0,7},{1,0},{2,1},{3,2},{4,3},{5,4},{6,5},{7,6},{8,15},{9,8},{10,9... | collective-permute-start | bytes 1916936 | tf_op jit(solution)/shard_map/ppermute | solution.py:24
  78.0 20.5 %copy-start.1 = (bf16[6656,128]{1,0:T(8,128)(2,1)S(1)}, bf16[6656,128]{1,0:T(8,128)(2,1)}, u32[]{:S(2)}) copy-start(bf16[6656,128]{1,0:T(8,128)(2,1)} %refs_9_.3) | copy-start | bytes 5111812
  78.0 20.5 %collective-permute-start.14 = (bf16[48,3328]{1,0:T(8,128)(2,1)S(1)}, bf16[48,3328]{1,0:T(8,128)(2,1)S(1)}, u32[]{:S(2)}, u32[]{:S(2)}) collective-permute-start(bf16[48,3328]{1,0:T(8,128)(2,1)S(1)} %half_of.6), channel_id=1, source_target_pairs={{0,1},{1,2},{2,3},{3,4},{4,5},{5,6},{6,7},{7,0},{8,9},{9,10},{10,1... | collective-permute-start | bytes 958472 | tf_op jit(solution)/shard_map/ppermute | solution.py:24
  78.1 20.4 %collective-permute-start.15 = (bf16[48,3328]{1,0:T(8,128)(2,1)S(1)}, bf16[48,3328]{1,0:T(8,128)(2,1)S(1)}, u32[]{:S(2)}, u32[]{:S(2)}) collective-permute-start(bf16[48,3328]{1,0:T(8,128)(2,1)S(1)} %half_of.7), channel_id=1, source_target_pairs={{0,7},{1,0},{2,1},{3,2},{4,3},{5,4},{6,5},{7,6},{8,15},{9,8},{10,9... | collective-permute-start | bytes 958472 | tf_op jit(solution)/shard_map/ppermute | solution.py:24
  91.7 12.8 %collective-permute-start.6 = (bf16[48,3328]{1,0:T(8,128)(2,1)S(1)}, bf16[48,3328]{1,0:T(8,128)(2,1)S(1)}, u32[]{:S(2)}, u32[]{:S(2)}) collective-permute-start(bf16[48,3328]{1,0:T(8,128)(2,1)S(1)} %half_of.4), channel_id=1, source_target_pairs={{0,1},{1,2},{2,3},{3,4},{4,5},{5,6},{6,7},{7,0},{8,9},{9,10},{10,1... | collective-permute-start | bytes 958472 | tf_op jit(solution)/shard_map/ppermute | solution.py:24
  92.0 12.5 %collective-permute-start.7 = (bf16[48,3328]{1,0:T(8,128)(2,1)S(1)}, bf16[48,3328]{1,0:T(8,128)(2,1)S(1)}, u32[]{:S(2)}, u32[]{:S(2)}) collective-permute-start(bf16[48,3328]{1,0:T(8,128)(2,1)S(1)} %half_of.5), channel_id=1, source_target_pairs={{0,7},{1,0},{2,1},{3,2},{4,3},{5,4},{6,5},{7,6},{8,15},{9,8},{10,9... | collective-permute-start | bytes 958472 | tf_op jit(solution)/shard_map/ppermute | solution.py:24
  110.0 23.6 %copy-start = (f32[1024]{0:T(1024)S(1)}, f32[1024]{0:T(1024)}, u32[]{:S(2)}) copy-start(f32[1024]{0:T(1024)} %param.6) | copy-start | bytes 12292
  110.1 1.9 %collective-permute-start.16 = (f32[912,128]{1,0:T(8,128)S(1)}, f32[912,128]{1,0:T(8,128)S(1)}, u32[]{:S(2)}, u32[]{:S(2)}) collective-permute-start(f32[912,128]{1,0:T(8,128)S(1)} %get-tuple-element.31), channel_id=1, source_target_pairs={{0,8},{8,0},{1,9},{9,1},{2,10},{10,2},{3,11},{11,3},{4,12},{12,4},... | collective-permute-start | bytes 1400840 | tf_op jit(solution)/shard_map/ppermute | solution.py:24
  112.1 7.8 %collective-permute-start.17 = (f32[336,128]{1,0:T(8,128)S(1)}, f32[336,128]{1,0:T(8,128)S(1)}, u32[]{:S(2)}, u32[]{:S(2)}) collective-permute-start(f32[336,128]{1,0:T(8,128)S(1)} %get-tuple-element.33), channel_id=1, source_target_pairs={{0,64},{64,128},{128,192},{192,0},{1,65},{65,129},{129,193},{193,1... | collective-permute-start | bytes 516104 | tf_op jit(solution)/shard_map/ppermute | solution.py:24
  113.8 11.0 %collective-permute-start.18 = (f32[336,128]{1,0:T(8,128)S(1)}, f32[336,128]{1,0:T(8,128)S(1)}, u32[]{:S(2)}, u32[]{:S(2)}) collective-permute-start(f32[336,128]{1,0:T(8,128)S(1)} %get-tuple-element.34), channel_id=1, source_target_pairs={{0,128},{64,192},{128,0},{192,64},{1,129},{65,193},{129,1},{193,65... | collective-permute-start | bytes 516104 | tf_op jit(solution)/shard_map/ppermute | solution.py:24
  116.7 8.1 %collective-permute-start.19 = (f32[336,128]{1,0:T(8,128)S(1)}, f32[336,128]{1,0:T(8,128)S(1)}, u32[]{:S(2)}, u32[]{:S(2)}) collective-permute-start(f32[336,128]{1,0:T(8,128)S(1)} %get-tuple-element.35), channel_id=1, source_target_pairs={{0,192},{64,0},{128,64},{192,128},{1,193},{65,1},{129,65},{193,129... | collective-permute-start | bytes 516104 | tf_op jit(solution)/shard_map/ppermute | solution.py:24
  124.8 5.1 %collective-permute-start.20 = (f32[192,128]{1,0:T(8,128)S(1)}, f32[192,128]{1,0:T(8,128)S(1)}, u32[]{:S(2)}, u32[]{:S(2)}) collective-permute-start(f32[192,128]{1,0:T(8,128)S(1)} %get-tuple-element.37), channel_id=1, source_target_pairs={{0,16},{16,32},{32,48},{48,0},{1,17},{17,33},{33,49},{49,1},{2,18}... | collective-permute-start | bytes 294920 | tf_op jit(solution)/shard_map/ppermute | solution.py:24
  125.3 7.1 %collective-permute-start.21 = (f32[192,128]{1,0:T(8,128)S(1)}, f32[192,128]{1,0:T(8,128)S(1)}, u32[]{:S(2)}, u32[]{:S(2)}) collective-permute-start(f32[192,128]{1,0:T(8,128)S(1)} %get-tuple-element.38), channel_id=1, source_target_pairs={{0,32},{16,48},{32,0},{48,16},{1,33},{17,49},{33,1},{49,17},{2,34}... | collective-permute-start | bytes 294920 | tf_op jit(solution)/shard_map/ppermute | solution.py:24
  127.8 5.8 %collective-permute-start.22 = (f32[192,128]{1,0:T(8,128)S(1)}, f32[192,128]{1,0:T(8,128)S(1)}, u32[]{:S(2)}, u32[]{:S(2)}) collective-permute-start(f32[192,128]{1,0:T(8,128)S(1)} %get-tuple-element.39), channel_id=1, source_target_pairs={{0,48},{16,0},{32,16},{48,32},{1,49},{17,1},{33,17},{49,33},{2,50}... | collective-permute-start | bytes 294920 | tf_op jit(solution)/shard_map/ppermute | solution.py:24
where the time goes:
time: 139 us; the launch traced here: 138 us
  waiting for transfers between devices  66.1 us (48%)
  starting transfers between devices  38.5 us (28%)
  Pallas kernels  16.6 us (12%)
  blocking collectives  14 us (10%)
  local copies, waits for them, and re-layouts  2.47 us (2%)
    ppermute x23, waiting for transfers between devices, shifted(): lax.ppermute(value, axis, [(i, (i + by) % size) for i in range(size)])  66.1 us
    ppermute x23, starting transfers between devices, shifted(): lax.ppermute(value, axis, [(i, (i + by) % size) for i in range(size)])  38.5 us
    all_to_all x1, blocking collectives, gathered_weights(): parts = lax.all_to_all(copies, DP, split_axis=0, concat_axis=0, tiled=True)  14 us
    pallas_call x2, Pallas kernels, chunk_step(): pl.pallas_call(kernel, out_shape=outs, in_specs=[HBM] * 10 + [VMEM] * (4...  11.4 us
    pallas_call x8, Pallas kernels, small_call(): pl.pallas_call(kernel, out_shape=outs, in_specs=[VMEM] * len(operands), o...  5.15 us
  transfers between devices with their start and end apart: 23, of which 13 were waited for; matrix products, arithmetic and copies ran while one was open for 1% of the time, Pallas kernels for 4%

commit v1 on v0

--- a/solution.py
+++ b/solution.py
@@ -14,7 +14,6 @@
 EPSILON = 1e-05
 CHUNKS = (26, 26)
 f32, bf16 = jnp.float32, jnp.bfloat16
-highest = lax.Precision.HIGHEST
 VMEM = pl.BlockSpec(memory_space=pltpu.VMEM)
 HBM = pl.BlockSpec(memory_space=pltpu.HBM)
 
@@ -47,7 +46,7 @@
 
 
 def sums_over_ring(chunks, starts, cot, shard):
-    weights = gathered_weights(shard).T
+    weights = gathered_weights(shard)
     sides = [([c], [c]) for c in chunks]
     for hop in range(3):
         for index, (r, l) in enumerate(sides):
@@ -56,124 +55,175 @@
             r.append(shifted(r[-1], "group", 1))
             l.append(shifted(l[-1], "group", -1))
     totals = None
-    for (r, l), start in zip(sides, starts):
-        far_r = shifted(half_of(r[3], True), "group", 1)
-        far_l = shifted(half_of(l[3], False), "group", -1)
-        parts = (r[0], r[1], r[2], r[3], l[1], l[2], l[3], far_r, far_l)
-        totals = chunk_step(parts, cot, start, weights, totals)
+    laid, fars = [], []
+    for r, l in sides:
+        if laid:
+            big, near, sx = laid[0]
+            r[3], l[3], sx = after(r[3], l[3], sx)
+            laid[0] = (big, near, sx)
+        fars.append(
+            (shifted(half_of(r[3], True), "group", 1), shifted(half_of(l[3], False), "group", -1))
+        )
+        laid.append(near_step((*r, *l[1:]), weights))
+    for (far_r, far_l), here, start in zip(fars, laid, starts):
+        totals = far_step(far_r, far_l, here, cot, start, weights, totals)
     return totals
 
 
 TILES = 2
 
 
-def chunk_kernel(*refs, start, accumulate):
-    own, r1, r2, r3, l1, l2, l3, fr, fl, cot, wt = refs[:11]
-    rest = refs[11:]
-    if accumulate:
-        ins, rest = rest[:3], rest[3:]
-    ab, hg, sx, big, ce, sems = rest
-    width, tokens = own.shape
-    half = width // 2
+def near_step(blocks, weights):
+    width, tokens = blocks[0].shape
+    channels = weights.shape[1]
+    rows = 8 * width
     tile = tokens // TILES
-    z = lax.axis_index("group")
+    ahead = (0, 7, 6, 5, 1, 2, 3)
+
+    def kernel(own, r1, r2, r3, l1, l2, l3, w, big, near, sx, sems):
+        z = lax.axis_index("group")
+        refs = (own, r1, r2, r3, l1, l2, l3)
+
+        def place(by):
+            return pl.ds(pl.multiple_of(((z + by) % 8) * width, 32), width)
+
+        moves = [
+            [
+                pltpu.make_async_copy(
+                    ref.at[:, step * tile : (step + 1) * tile],
+                    big.at[step, place(by), :],
+                    sems.at[step, index],
+                )
+                for index, (ref, by) in enumerate(zip(refs, ahead))
+            ]
+            for step in range(TILES)
+        ]
+        for step in moves:
+            for move in step:
+                move.start()
+        for step in range(TILES):
+            big[step, place(4), :] = jnp.zeros((width, tile), bf16)
+            big[step, rows + channels :, :] = jnp.ones((16, tile), bf16)
+        wt = w[...].astype(f32).T.astype(bf16)
+        sx[place(4), :] = jnp.zeros((width, channels), f32)
+        for ref, by in zip(refs, ahead):
+            total = jnp.sum(ref[...].astype(f32), axis=1, keepdims=True)
+            sx[place(by), :] = jnp.broadcast_to(total, (width, channels))
+        for step in range(TILES):
+            for move in moves[step]:
+                move.wait()
+            near[step] = jnp.dot(wt, big[step, :rows, :], preferred_element_type=f32)
+
+    return pl.pallas_call(
+        kernel,
+        out_shape=(
+            jax.ShapeDtypeStruct((TILES, rows + channels + 16, tile), bf16),
+            jax.ShapeDtypeStruct((TILES, channels, tile), f32),
+            jax.ShapeDtypeStruct((rows, channels), f32),
+        ),
+        in_specs=[VMEM] * 8,
+        out_specs=(VMEM,) * 3,
+        scratch_shapes=[pltpu.SemaphoreType.DMA((TILES, 7))],
+        cost_estimate=pl.CostEstimate(
+            flops=2 * tokens * rows * channels, bytes_accessed=2 * tokens * rows, transcendentals=0
+        ),
+        compiler_params=pltpu.CompilerParams(vmem_limit_bytes=14 * 1024 * 1024),
+        name="near",
+    )(*blocks, weights)
+
+
+def far_step(far_r, far_l, laid, cot, start, weights, totals):
+    half, tokens = far_r.shape
+    width = 2 * half
     channels = cot.shape[1]
     rows = 8 * width
-    blocks = (
-        (own, 0, 0),
-        (r1, 7, 0),
-        (l1, 1, 0),
-        (r2, 6, 0),
-        (l2, 2, 0),
-        (r3, 5, 0),
-        (l3, 3, 0),
-        (fr, 4, 0),
-        (fl, 4, half),
-    )
-
-    def copies(step):
-        found = []
-        for index, (ref, ahead, extra) in enumerate(blocks):
-            row = pl.multiple_of(((z + ahead) % 8) * width + extra, 16)
-            found.append(
+    tile = tokens // TILES
+    accumulate = totals is not None
+
+    def kernel(*refs):
+        far_r, far_l, big_in, near, near_sx, cot, w = refs[:7]
+        ins, rest = (refs[7:10], refs[10:]) if accumulate else ((), refs[7:])
+        big, ab, hg, sx, ce, sems = rest
+        row = pl.multiple_of(((lax.axis_index("group") + 4) % 8) * width, 32)
+
+        moves = [
+            [
                 pltpu.make_async_copy(
-                    ref.at[:, step * tile : (step + 1) * tile],
-                    big.at[step, pl.ds(row, ref.shape[0]), :],
-                    sems.at[step, index],
-                )
-            )
-        found.append(
-            pltpu.make_async_copy(
-                cot.at[start + step * tile : start + (step + 1) * tile, :],
-                ce.at[step, :, :channels],
-                sems.at[step, len(blocks)],
-            )
+                    far_r.at[:, step * tile : (step + 1) * tile],
+                    big.at[step, pl.ds(row, half), :],
+                    sems.at[step, 0],
+                ),
+                pltpu.make_async_copy(
+                    far_l.at[:, step * tile : (step + 1) * tile],
+                    big.at[step, pl.ds(pl.multiple_of(row + half, 16), half), :],
+                    sems.at[step, 1],
+                ),
+                pltpu.make_async_copy(
+                    cot.at[start + step * tile : start + (step + 1) * tile, :],
+                    ce.at[step, :, :channels],
+                    sems.at[step, 2],
+                ),
+            ]
+            for step in range(TILES)
+        ]
+        for step in moves:
+            for move in step:
+                move.start()
+        w_far = w[pl.ds(row, width), :].astype(f32).T.astype(bf16)
+        far_sx = jnp.concatenate(
+            [
+                jnp.sum(ref[...].astype(f32), axis=1, keepdims=True)
+                for ref in (far_r, far_l)
+            ],
+            axis=0,
         )
-        return found
-
-    moves = [copies(step) for step in range(TILES)]
-    for step in moves:
-        for move in step:
-            move.start()
-    for step in range(TILES):
-        big[step, rows + channels :, :] = jnp.ones((16, tile), bf16)
-    for step in range(TILES):
-        for move in moves[step]:
-            move.wait()
-        et = jnp.dot(wt[...], big[step, :rows, :], preferred_element_type=f32)
-        big[step, rows : rows + channels, :] = et.astype(bf16)
-        ce[step, :, channels:] = et.T.astype(bf16)
-        product = jnp.dot(big[step], ce[step], preferred_element_type=f32)
-        sums = lax.dot_general(
-            jnp.ones((8, tile), bf16),
-            big[step, :rows, :],
-            (((1,), (1,)), ((), ())),
-            preferred_element_type=f32,
-        )
-        if step or accumulate:
-            before = (ab, hg, sx) if step else ins
-            ab[...] = before[0][...] + product[:rows]
-            hg[...] = before[1][...] + product[rows : rows + channels + 8]
-            sx[...] = before[2][...] + sums
-        else:
-            ab[...] = product[:rows]
-            hg[...] = product[rows : rows + channels + 8]
-            sx[...] = sums
-
-
-def chunk_step(parts, cot, start, wt, totals):
-    width, tokens = parts[0].shape
-    channels = cot.shape[1]
-    rows = 8 * width
-    outs = (
-        jax.ShapeDtypeStruct((rows, 2 * channels), f32),
-        jax.ShapeDtypeStruct((channels + 8, 2 * channels), f32),
-        jax.ShapeDtypeStruct((8, rows), f32),
-    )
-    accumulate = totals is not None
-
-    def kernel(*refs):
-        chunk_kernel(*refs, start=start, accumulate=accumulate)
-
-    return pl.pallas_call(
+        sums = near_sx[...] + ins[2][...] if accumulate else near_sx[...]
+        sx[...] = sums
+        sx[pl.ds(row, width), :] = sx[pl.ds(row, width), :] + far_sx
+        for step in range(TILES):
+            for move in moves[step]:
+                move.wait()
+            et = near[step] + jnp.dot(
+                w_far, big[step, pl.ds(row, width), :], preferred_element_type=f32
+            )
+            big[step, rows : rows + channels, :] = et.astype(bf16)
+            ce[step, :, channels:] = et.T.astype(bf16)
+            product = jnp.dot(big[step], ce[step], preferred_element_type=f32)
+            if step or accumulate:
+                before = (ab, hg) if step else ins
+                ab[...] = before[0][...] + product[:rows]
+                hg[...] = before[1][...] + product[rows : rows + channels + 8]
+            else:
+                ab[...] = product[:rows]
+                hg[...] = product[rows : rows + channels + 8]
+
+    aliases = {2: 0}
+    if accumulate:
+        aliases.update({7: 1, 8: 2, 9: 3})
+    outs = pl.pallas_call(
         kernel,
-        out_shape=outs,
-        in_specs=[HBM] * 10 + [VMEM] * (4 if accumulate else 1),
-        out_specs=(VMEM, VMEM, VMEM),
+        out_shape=(
+            jax.ShapeDtypeStruct(laid[0].shape, bf16),
+            jax.ShapeDtypeStruct((rows, 2 * channels), f32),
+            jax.ShapeDtypeStruct((channels + 8, 2 * channels), f32),
+            jax.ShapeDtypeStruct((rows, channels), f32),
+        ),
+        in_specs=[VMEM] * 5 + [HBM] + [VMEM] * (4 if accumulate else 1),
+        out_specs=(VMEM,) * 4,
         scratch_shapes=[
-            pltpu.VMEM((TILES, rows + channels + 16, tokens // TILES), bf16),
-            pltpu.VMEM((TILES, tokens // TILES, 2 * channels), bf16),
-            pltpu.SemaphoreType.DMA((TILES, 10)),
+            pltpu.VMEM((TILES, tile, 2 * channels), bf16),
+            pltpu.SemaphoreType.DMA((TILES, 3)),
         ],
-        input_output_aliases={11: 0, 12: 1, 13: 2} if accumulate else {},
+        input_output_aliases=aliases,
         cost_estimate=pl.CostEstimate(
-            flops=2 * tokens * (rows * 3 * channels + channels * 2 * channels),
+            flops=2 * tokens * (rows + channels) * 2 * channels,
             bytes_accessed=2 * tokens * rows,
             transcendentals=0,
         ),
-        compiler_params=pltpu.CompilerParams(vmem_limit_bytes=12 * 1024 * 1024),
-        name="chunk",
-    )(*parts, cot, wt, *(totals or ()))
+        compiler_params=pltpu.CompilerParams(vmem_limit_bytes=14 * 1024 * 1024),
+        name="far",
+    )(far_r, far_l, *laid, cot, weights, *(totals or ()))
+    return outs[1:]
 
 
 def small_call(kernel, outs, operands, name):
@@ -188,7 +238,7 @@
     )(*operands)
 
 
-COMMON = 144
+COMMON = 112
 
 
 def core_stage(totals):
@@ -206,23 +256,38 @@
                     ref[to : to + share, :] = ab[
                         pl.ds(row, share), side * channels : (side + 1) * channels
                     ]
-            low = lax.broadcasted_iota(jnp.int32, (GW, channels), 1) < GW
+            lane = lax.broadcasted_iota(jnp.int32, (GW, channels), 1)
+            row = lax.broadcasted_iota(jnp.int32, (GW, channels), 0)
+            low = lane < GW
+            mixed, gram = (
+                jnp.where(low, hg[:GW, cols], hg[GW : 2 * GW, cols])
+                for cols in (slice(0, channels), slice(channels, 2 * channels))
+            )
             base = 32 * share
+            ref[base : base + GW, :] = mixed
+            square = jnp.where(row < lane, gram, pltpu.roll(gram, GW, 1))
+            ref[base + GW : base + GW + 32, :] = jnp.where(
+                low[:32], square[:32], pltpu.roll(square, GW, 1)[32:]
+            )
+            base += GW + 32
+            ref[base : base + 16, :] = jnp.zeros((16, channels), f32)
+            diagonal = (lane == row) | (lane == row + GW)
+            square_eye = lax.broadcasted_iota(
+                jnp.int32, (channels, channels), 0
+            ) == lax.broadcasted_iota(jnp.int32, (channels, channels), 1)
+            ref[base : base + 1, :] = jnp.sum(
+                jnp.where(diagonal, gram, 0.0), axis=0, keepdims=True
+            )
             for side in range(2):
-                cols = slice(side * channels, (side + 1) * channels)
-                ref[base + side * GW : base + (side + 1) * GW, :] = jnp.where(
-                    low, hg[:GW, cols], hg[GW : 2 * GW, cols]
-                )
-            base += 2 * GW
-            ref[base : base + COMMON - 2 * GW, :] = jnp.zeros((COMMON - 2 * GW, channels), f32)
-            for side in range(2):
-                ref[base + side : base + side + 1, :] = hg[
+                ref[base + 1 + side : base + 2 + side, :] = hg[
                     2 * GW : 2 * GW + 1, side * channels : (side + 1) * channels
                 ]
             for part in range(6):
-                ref[base + 8 + part : base + 9 + part, :] = sx[
-                    0:1, part * channels : (part + 1) * channels
-                ]
+                ref[base + 3 + part : base + 4 + part, :] = jnp.sum(
+                    jnp.where(square_eye, sx[part * channels : (part + 1) * channels, :], 0.0),
+                    axis=0,
+                    keepdims=True,
+                )
 
     shape = jax.ShapeDtypeStruct((32 * share + COMMON, channels), f32)
     return small_call(kernel, (shape, shape), (ab, hg, sx), "core_stage")
@@ -249,8 +314,19 @@
     return small_call(kernel, (shape,) * 4, received, "axis_stage")
 
 
+def split(value):
+    high = value.astype(bf16)
+    return high, (value - high.astype(f32)).astype(bf16)
+
+
 def dot(left, right):
-    return jnp.dot(left, right, preferred_element_type=f32, precision=highest)
+    left_high, left_low = split(left)
+    right_high, right_low = split(right)
+    both = jnp.concatenate([left_high, left_low], axis=1)
+    twice = jnp.concatenate([right_high, right_high], axis=0)
+    return jnp.dot(both, twice, preferred_element_type=f32) + jnp.dot(
+        left_high, right_low, preferred_element_type=f32
+    )
 
 
 def last_stage(received, gain, total_tokens):
@@ -286,11 +362,20 @@
             return jnp.sum(eye * line, axis=1, keepdims=True)
 
         h_t = blocks(everything[base : base + GW])
-        gram = blocks(everything[base + GW : base + 2 * GW])
-        base += 2 * GW
-        cot_sum = everything[base : base + 1]
-        mean = everything[base + 1 : base + 2] * inverse
-        patch_sums = everything[base + 8 : base + 14]
+        packed = everything[base + GW : base + GW + 32]
+        square = jnp.concatenate([packed, pltpu.roll(packed, GW, 1)], axis=0)
+        square = jnp.where(lane[:GW] < GW, square, 0.0)
+        square = jnp.concatenate([square, jnp.zeros((GW, channels), f32)], axis=0)
+        turned = square.T
+        upper = jnp.where(row < lane, square, turned)
+        lower = jnp.where(row > lane, square, turned)
+        lower = pltpu.roll(jnp.concatenate([lower[GW:], lower[:GW]], axis=0), GW, 1)
+        base += GW + 32
+        gram = jnp.where(row < GW, upper, lower)
+        gram = jnp.where(same & (lane != row), gram, 0.0) + eye * everything[base : base + 1]
+        cot_sum = everything[base + 1 : base + 2]
+        mean = everything[base + 2 : base + 3] * inverse
+        patch_sums = everything[base + 3 : base + 9]
         mean_col = column(mean)
         covariance = gram * inverse - jnp.where(same, mean_col * mean, 0.0) + EPSILON * eye
         h_t = h_t - jnp.where(same, mean_col * cot_sum, 0.0)

time: 139 us -> 138 us (level)
  blocking collectives: 14 us -> 0 us
  starting transfers between devices: 38.5 us -> 45 us
  waiting for transfers between devices: 66.1 us -> 70.5 us
  Pallas kernels: 16.6 us -> 19.5 us
    all_to_all x1 -> x0, blocking collectives: 14 us -> none  [gathered_weights(): parts = lax.all_to_all(copies, DP, split_axis=0, concat_axis=0, tiled=True)]
    all_to_all x0 -> x1, starting transfers between devices: none -> 7.56 us  [gathered_weights(): parts = lax.all_to_all(copies, DP, split_axis=0, concat_axis=0, tiled=True)]
    pallas_call x2 -> x4, Pallas kernels: 11.4 us -> 15.9 us  [the longest x2 9.45 us: far_step(): pl.pallas_call(kernel, out_shape=(jax.ShapeDtypeStruct(laid[0].shape, bf1...]
    ppermute x23, waiting for transfers between devices: 66.1 us -> 70.5 us  [shifted(): lax.ppermute(value, axis, [(i, (i + by) % size) for i in range(size)])]
    pallas_call x8, Pallas kernels: 5.15 us -> 3.56 us  [small_call(): pl.pallas_call(kernel, out_shape=outs, in_specs=[VMEM] * len(operands), o...]
  transfers between devices with their start and end apart: 23 -> 24, of which waited for: 13 -> 16; matrix products, arithmetic and copies ran while one was open for 1% -> 1% of each run, Pallas kernels for 4% -> 8%
where the time goes in v1:
time: 138 us
  waiting for transfers between devices  70.5 us (51%)
  starting transfers between devices  45 us (33%)
  Pallas kernels  19.5 us (14%)
  local copies, waits for them, and re-layouts  2.09 us (2%)
    ppermute x23, waiting for transfers between devices, shifted(): lax.ppermute(value, axis, [(i, (i + by) % size) for i in range(size)])  70.5 us
    ppermute x23, starting transfers between devices, shifted(): lax.ppermute(value, axis, [(i, (i + by) % size) for i in range(size)])  37.4 us
    pallas_call x2, Pallas kernels, far_step(): pl.pallas_call(kernel, out_shape=(jax.ShapeDtypeStruct(laid[0].shape, bf1...  9.45 us
    all_to_all x1, starting transfers between devices, gathered_weights(): parts = lax.all_to_all(copies, DP, split_axis=0, concat_axis=0, tiled=True)  7.56 us
    pallas_call x2, Pallas kernels, near_step(): pl.pallas_call(kernel, out_shape=(jax.ShapeDtypeStruct((TILES, rows + cha...  6.47 us
    pallas_call x8, Pallas kernels, small_call(): pl.pallas_call(kernel, out_shape=outs, in_specs=[VMEM] * len(operands), o...  3.56 us
  transfers between devices with their start and end apart: 24, of which 16 were waited for; matrix products, arithmetic and copies ran while one was open for 1% of the time, Pallas kernels for 8%

profile of v1, /device:TPU:6, one launch (start us, length us, event | category | flops | bytes accessed | tf_op | source)
XLA Modules:
  0.0 137.8 jit_solution(11215230229332703405)
XLA Ops:
  0.6 1.4 fusion
  2.0 5.9 %collective-permute-start.9 = (bf16[96,3328]{1,0:T(8,128)(2,1)S(1)}, bf16[96,3328]{1,0:T(8,128)(2,1)S(1)}, u32[]{:S(2)}, u32[]{:S(2)}) collective-permute-start(bf16[96,3328]{1,0:T(8,128)(2,1)S(1)} %get-tuple-element.60.own), channel_id=1, source_target_pairs={{0,7},{1,0},{2,1},{3,2},{4,3},{5,4},{6,5},{7,6},{8,15},{9,8},{10,9... | collective-permute-start | bytes 1916936 | tf_op jit(solution)/shard_map/ppermute | solution.py:23
  7.9 0.0 collective-permute-start.6
  7.9 0.0 collective-permute-start
  7.9 3.3 %collective-permute-start.3 = (bf16[96,3328]{1,0:T(8,128)(2,1)S(1)}, bf16[96,3328]{1,0:T(8,128)(2,1)S(1)}, u32[]{:S(2)}, u32[]{:S(2)}) collective-permute-start(bf16[96,3328]{1,0:T(8,128)(2,1)S(1)} %get-tuple-element.61.own), channel_id=1, source_target_pairs={{0,7},{1,0},{2,1},{3,2},{4,3},{5,4},{6,5},{7,6},{8,15},{9,8},{10,9... | collective-permute-start | bytes 1916936 | tf_op jit(solution)/shard_map/ppermute | solution.py:23
  11.2 0.7 broadcast_in_dim.3
  11.9 7.6 %all-to-all-start = ((bf16[32,24,128]{2,1,0:T(8,128)(2,1)}), bf16[32,24,128]{2,1,0:T(8,128)(2,1)S(1)}, u32[]{:S(2)}, u32[]{:S(2)}) async-start(bf16[32,24,128]{2,1,0:T(8,128)(2,1)} %broadcast_in_dim.3), calls=%async_computation | async-start | bytes 393216 | tf_op jit(solution)/shard_map/all_to_all | solution.py:29
  19.5 3.2 %collective-permute-done.9.l1 = bf16[96,3328]{1,0:T(8,128)(2,1)S(1)} collective-permute-done((bf16[96,3328]{1,0:T(8,128)(2,1)S(1)}, bf16[96,3328]{1,0:T(8,128)(2,1)S(1)}, u32[]{:S(2)}, u32[]{:S(2)}) %collective-permute-start.9) | collective-permute-done | bytes 639008 | tf_op jit(solution)/shard_map/ppermute | solution.py:23
  22.7 3.7 %collective-permute-start.10 = (bf16[96,3328]{1,0:T(8,128)(2,1)S(1)}, bf16[96,3328]{1,0:T(8,128)(2,1)}, u32[]{:S(2)}, u32[]{:S(2)}) collective-permute-start(bf16[96,3328]{1,0:T(8,128)(2,1)S(1)} %collective-permute-done.9.l1), channel_id=1, source_target_pairs={{0,7},{1,0},{2,1},{3,2},{4,3},{5,4},{6,5},{7,6},{8,15},{9,8},{10,9... | collective-permute-start | bytes 1916936 | tf_op jit(solution)/shard_map/ppermute | solution.py:23
  26.4 0.1 collective-permute-done.6.r1
  26.5 13.6 %collective-permute-done.r1 = bf16[96,3328]{1,0:T(8,128)(2,1)S(1)} collective-permute-done((bf16[96,3328]{1,0:T(8,128)(2,1)S(1)}, bf16[96,3328]{1,0:T(8,128)(2,1)S(1)}, u32[]{:S(2)}, u32[]{:S(2)}) %collective-permute-start) | collective-permute-done | bytes 639008 | tf_op jit(solution)/shard_map/ppermute | solution.py:23
  40.1 0.0 collective-permute-done.3.l1
  40.1 0.0 collective-permute-start.4
  40.1 2.0 %collective-permute-start.1 = (bf16[96,3328]{1,0:T(8,128)(2,1)S(1)}, bf16[96,3328]{1,0:T(8,128)(2,1)S(1)}, u32[]{:S(2)}, u32[]{:S(2)}) collective-permute-start(bf16[96,3328]{1,0:T(8,128)(2,1)S(1)} %collective-permute-done.r1), channel_id=1, source_target_pairs={{0,1},{1,2},{2,3},{3,4},{4,5},{5,6},{6,7},{7,0},{8,9},{9,10},{10,1... | collective-permute-start | bytes 1916936 | tf_op jit(solution)/shard_map/ppermute | solution.py:23
  42.1 8.0 %collective-permute-done.10.l2 = bf16[96,3328]{1,0:T(8,128)(2,1)} collective-permute-done((bf16[96,3328]{1,0:T(8,128)(2,1)S(1)}, bf16[96,3328]{1,0:T(8,128)(2,1)}, u32[]{:S(2)}, u32[]{:S(2)}) %collective-permute-start.10) | collective-permute-done | bytes 639008 | tf_op jit(solution)/shard_map/ppermute | solution.py:23
  50.1 3.8 %collective-permute-start.11 = (bf16[96,3328]{1,0:T(8,128)(2,1)}, bf16[96,3328]{1,0:T(8,128)(2,1)S(1)}, u32[]{:S(2)}, u32[]{:S(2)}) collective-permute-start(bf16[96,3328]{1,0:T(8,128)(2,1)} %collective-permute-done.10.l2), channel_id=1, source_target_pairs={{0,7},{1,0},{2,1},{3,2},{4,3},{5,4},{6,5},{7,6},{8,15},{9,8},{10,9... | collective-permute-start | bytes 1916936 | tf_op jit(solution)/shard_map/ppermute | solution.py:23
  53.9 9.9 %collective-permute-done.4.l2 = bf16[96,3328]{1,0:T(8,128)(2,1)S(1)} collective-permute-done((bf16[96,3328]{1,0:T(8,128)(2,1)S(1)}, bf16[96,3328]{1,0:T(8,128)(2,1)S(1)}, u32[]{:S(2)}, u32[]{:S(2)}) %collective-permute-start.4) | collective-permute-done | bytes 639008 | tf_op jit(solution)/shard_map/ppermute | solution.py:23
  63.8 3.7 %collective-permute-start.5 = (bf16[96,3328]{1,0:T(8,128)(2,1)S(1)}, bf16[96,3328]{1,0:T(8,128)(2,1)S(1)}, u32[]{:S(2)}, u32[]{:S(2)}) collective-permute-start(bf16[96,3328]{1,0:T(8,128)(2,1)S(1)} %collective-permute-done.4.l2), channel_id=1, source_target_pairs={{0,7},{1,0},{2,1},{3,2},{4,3},{5,4},{6,5},{7,6},{8,15},{9,8},{10,9... | collective-permute-start | bytes 1916936 | tf_op jit(solution)/shard_map/ppermute | solution.py:23
  67.5 10.1 %collective-permute-done.11.l3.ref = bf16[96,3328]{1,0:T(8,128)(2,1)S(1)} collective-permute-done((bf16[96,3328]{1,0:T(8,128)(2,1)}, bf16[96,3328]{1,0:T(8,128)(2,1)S(1)}, u32[]{:S(2)}, u32[]{:S(2)}) %collective-permute-start.11) | collective-permute-done | bytes 639008 | tf_op jit(solution)/shard_map/ppermute | solution.py:23
  77.6 3.7 %collective-permute-start.15 = (bf16[48,3328]{1,0:T(8,128)(2,1)S(1)}, bf16[48,3328]{1,0:T(8,128)(2,1)S(1)}, u32[]{:S(2)}, u32[]{:S(2)}) collective-permute-start(bf16[48,3328]{1,0:T(8,128)(2,1)S(1)} %half_of.7), channel_id=1, source_target_pairs={{0,7},{1,0},{2,1},{3,2},{4,3},{5,4},{6,5},{7,6},{8,15},{9,8},{10,9... | collective-permute-start | bytes 958472 | tf_op jit(solution)/shard_map/ppermute | solution.py:23
  81.3 0.3 collective-permute-start.14
  81.6 4.0 %near.2 = (bf16[2,912,1664]{2,1,0:T(8,128)(2,1)S(1)}, f32[2,128,1664]{2,1,0:T(8,128)S(1)}, f32[768,128]{1,0:T(8,128)S(1)}) custom-call(bf16[96,3328]{1,0:T(8,128)(2,1)S(1)} %get-tuple-element.60.own, bf16[96,3328]{1,0:T(8,128)(2,1)} %collective-permute-done.6.r1, bf16[96,3328]{1,0:T(8,128)(2,1)} %collective-permute-done.7.r2, ...), custom_call_target="tpu_custom_call" | custom-call | flops 654311424 | bytes 5111808 | tf_op jit(solution)/shard_map/near/pallas_call | solution.py:117
  85.6 5.6 %collective-permute-done.5.ref.l3 = bf16[96,3328]{1,0:T(8,128)(2,1)S(1)} collective-permute-done((bf16[96,3328]{1,0:T(8,128)(2,1)S(1)}, bf16[96,3328]{1,0:T(8,128)(2,1)S(1)}, u32[]{:S(2)}, u32[]{:S(2)}) %collective-permute-start.5) | collective-permute-done | bytes 639008 | tf_op jit(solution)/shard_map/ppermute | solution.py:23
  91.2 3.7 %collective-permute-done.2.ref.r3 = bf16[96,3328]{1,0:T(8,128)(2,1)S(1)} collective-permute-done((bf16[96,3328]{1,0:T(8,128)(2,1)S(1)}, bf16[96,3328]{1,0:T(8,128)(2,1)S(1)}, u32[]{:S(2)}, u32[]{:S(2)}) %collective-permute-start.2) | collective-permute-done | bytes 639008 | tf_op jit(solution)/shard_map/ppermute | solution.py:23
  94.9 0.0 copy-start
  94.9 0.1 collective-permute-start.13
  95.0 2.0 %collective-permute-start.12 = (bf16[48,3328]{1,0:T(8,128)(2,1)S(1)}, bf16[48,3328]{1,0:T(8,128)(2,1)S(1)}, u32[]{:S(2)}, u32[]{:S(2)}) collective-permute-start(bf16[48,3328]{1,0:T(8,128)(2,1)S(1)} %half_of.4), channel_id=1, source_target_pairs={{0,1},{1,2},{2,3},{3,4},{4,5},{5,6},{6,7},{7,0},{8,9},{9,10},{10,1... | collective-permute-start | bytes 958472 | tf_op jit(solution)/shard_map/ppermute | solution.py:23
  97.0 2.5 %near.3 = (bf16[2,912,1664]{2,1,0:T(8,128)(2,1)S(1)}, f32[2,128,1664]{2,1,0:T(8,128)S(1)}, f32[768,128]{1,0:T(8,128)S(1)}) custom-call(bf16[96,3328]{1,0:T(8,128)(2,1)S(1)} %get-tuple-element.61.own, bf16[96,3328]{1,0:T(8,128)(2,1)S(1)} %collective-permute-done.r1, bf16[96,3328]{1,0:T(8,128)(2,1)S(1)} %collective-permute-done.1.r2, ...), custom_call_target="tpu_custom_call" | custom-call | flops 654311424 | bytes 5111808 | tf_op jit(solution)/shard_map/near/pallas_call | solution.py:117
  99.6 2.2 %collective-permute-done.14.refs_0_ = bf16[48,3328]{1,0:T(8,128)(2,1)S(1)} collective-permute-done((bf16[48,3328]{1,0:T(8,128)(2,1)S(1)}, bf16[48,3328]{1,0:T(8,128)(2,1)S(1)}, u32[]{:S(2)}, u32[]{:S(2)}) %collective-permute-start.14) | collective-permute-done | bytes 319520 | tf_op jit(solution)/shard_map/ppermute | solution.py:23
  101.7 4.7 %far.2 = (bf16[2,912,1664]{2,1,0:T(8,128)(2,1)S(1)}, f32[768,256]{1,0:T(8,128)S(1)}, f32[136,256]{1,0:T(8,128)S(1)}, f32[768,128]{1,0:T(8,128)S(1)}) custom-call(bf16[48,3328]{1,0:T(8,128)(2,1)S(1)} %collective-permute-done.14.refs_0_, bf16[48,3328]{1,0:T(8,128)(2,1)S(1)} %collective-permute-done.15.refs_1_, ...), custom_call_target="tpu_custom_call", output_to_operand_aliasing={{0}: (2, {})} | custom-call | flops 1526726656 | bytes 5111808 | tf_op jit(solution)/shard_map/far/pallas_call | solution.py:203
  106.4 0.7 collective-permute-done.12.refs_0_
  107.1 4.7 %far.3 = (bf16[2,912,1664]{2,1,0:T(8,128)(2,1)S(1)}, f32[768,256]{1,0:T(8,128)S(1)}, f32[136,256]{1,0:T(8,128)S(1)}, f32[768,128]{1,0:T(8,128)S(1)}) custom-call(bf16[48,3328]{1,0:T(8,128)(2,1)S(1)} %collective-permute-done.12.refs_0_, ...), custom_call_target="tpu_custom_call", output_to_operand_aliasing={{0}: (2, {}), {1}: (7, {}), {2}: (8, {}), {3}: (9, {})} | custom-call | flops 1526726656 | bytes 5111808 | tf_op jit(solution)/shard_map/far/pallas_call | solution.py:203
  111.9 0.0 copy-start.1
  111.9 0.2 core_stage.1
  112.1 0.1 collective-permute-start.16
  112.2 1.8 %collective-permute-done.16.refs_1_ = f32[880,128]{1,0:T(8,128)S(1)} collective-permute-done((f32[880,128]{1,0:T(8,128)S(1)}, f32[880,128]{1,0:T(8,128)S(1)}, u32[]{:S(2)}, u32[]{:S(2)}) %collective-permute-start.16) | collective-permute-done | bytes 450592 | tf_op jit(solution)/shard_map/ppermute | solution.py:23
  114.0 0.1 axis_stage.2
  114.0 1.7 %collective-permute-start.17 = (f32[304,128]{1,0:T(8,128)S(1)}, f32[304,128]{1,0:T(8,128)S(1)}, u32[]{:S(2)}, u32[]{:S(2)}) collective-permute-start(f32[304,128]{1,0:T(8,128)S(1)} %get-tuple-element.51), channel_id=1, source_target_pairs={{0,64},{64,128},{128,192},{192,0},{1,65},{65,129},{129,193},{193,1... | collective-permute-start | bytes 466952 | tf_op jit(solution)/shard_map/ppermute | solution.py:23
  115.7 2.9 %collective-permute-start.18 = (f32[304,128]{1,0:T(8,128)S(1)}, f32[304,128]{1,0:T(8,128)S(1)}, u32[]{:S(2)}, u32[]{:S(2)}) collective-permute-start(f32[304,128]{1,0:T(8,128)S(1)} %get-tuple-element.52), channel_id=1, source_target_pairs={{0,128},{64,192},{128,0},{192,64},{1,129},{65,193},{129,1},{193,65... | collective-permute-start | bytes 466952 | tf_op jit(solution)/shard_map/ppermute | solution.py:23
  118.6 1.3 collective-permute-start.19
  119.9 1.5 %collective-permute-done.17.refs_1_ = f32[304,128]{1,0:T(8,128)S(1)} collective-permute-done((f32[304,128]{1,0:T(8,128)S(1)}, f32[304,128]{1,0:T(8,128)S(1)}, u32[]{:S(2)}, u32[]{:S(2)}) %collective-permute-start.17) | collective-permute-done | bytes 155680 | tf_op jit(solution)/shard_map/ppermute | solution.py:23
  121.4 4.5 %collective-permute-done.18.refs_2_ = f32[304,128]{1,0:T(8,128)S(1)} collective-permute-done((f32[304,128]{1,0:T(8,128)S(1)}, f32[304,128]{1,0:T(8,128)S(1)}, u32[]{:S(2)}, u32[]{:S(2)}) %collective-permute-start.18) | collective-permute-done | bytes 155680 | tf_op jit(solution)/shard_map/ppermute | solution.py:23
  126.0 0.6 collective-permute-start.20
  126.5 2.4 %collective-permute-start.21 = (f32[160,128]{1,0:T(8,128)S(1)}, f32[160,128]{1,0:T(8,128)S(1)}, u32[]{:S(2)}, u32[]{:S(2)}) collective-permute-start(f32[160,128]{1,0:T(8,128)S(1)} %get-tuple-element.56), channel_id=1, source_target_pairs={{0,32},{16,48},{32,0},{48,16},{1,33},{17,49},{33,1},{49,17},{2,34}... | collective-permute-start | bytes 245768 | tf_op jit(solution)/shard_map/ppermute | solution.py:23
  129.0 1.6 %collective-permute-done.20.refs_1_ = f32[160,128]{1,0:T(8,128)S(1)} collective-permute-done((f32[160,128]{1,0:T(8,128)S(1)}, f32[160,128]{1,0:T(8,128)S(1)}, u32[]{:S(2)}, u32[]{:S(2)}) %collective-permute-start.20) | collective-permute-done | bytes 81952 | tf_op jit(solution)/shard_map/ppermute | solution.py:23
  130.6 2.7 %collective-permute-done.21.refs_2_ = f32[160,128]{1,0:T(8,128)S(1)} collective-permute-done((f32[160,128]{1,0:T(8,128)S(1)}, f32[160,128]{1,0:T(8,128)S(1)}, u32[]{:S(2)}, u32[]{:S(2)}) %collective-permute-start.21) | collective-permute-done | bytes 81952 | tf_op jit(solution)/shard_map/ppermute | solution.py:23
  133.3 1.3 collective-permute-done.22.refs_3_
  134.6 3.2 %last_stage.1 = (f32[24,128]{1,0:T(8,128)}, f32[1,128]{1,0:T(1,128)}) custom-call(f32[160,128]{1,0:T(8,128)S(1)} %get-tuple-element.54.refs_0_, f32[160,128]{1,0:T(8,128)S(1)} %collective-permute-done.20.refs_1_, f32[160,128]{1,0:T(8,128)S(1)} %collective-permute-done.21.refs_2_, f32[160,128]{1,0:T(8,128)S(1)} %collective-permute-done.22.refs_3_, ...), custom_call_target="tpu_custom_call" | custom-call | flops 1000000 | bytes 1000000 | tf_op jit(solution)/shard_map/last_stage/pallas_call | solution.py:230
  (20 shorter events, 0.2 us)
Async XLA Ops:
  0.6 10.6 %copy-start.2 = (bf16[24,128]{1,0:T(8,128)(2,1)S(1)}, bf16[24,128]{1,0:T(8,128)(2,1)}, u32[]{:S(2)}) copy-start(bf16[24,128]{1,0:T(8,128)(2,1)} %param.5) | copy-start | bytes 18436
  2.0 20.7 %collective-permute-start.9 = (bf16[96,3328]{1,0:T(8,128)(2,1)S(1)}, bf16[96,3328]{1,0:T(8,128)(2,1)S(1)}, u32[]{:S(2)}, u32[]{:S(2)}) collective-permute-start(bf16[96,3328]{1,0:T(8,128)(2,1)S(1)} %get-tuple-element.60.own), channel_id=1, source_target_pairs={{0,7},{1,0},{2,1},{3,2},{4,3},{5,4},{6,5},{7,6},{8,15},{9,8},{10,9... | collective-permute-start | bytes 1916936 | tf_op jit(solution)/shard_map/ppermute | solution.py:23
  7.9 18.6 %collective-permute-start.6 = (bf16[96,3328]{1,0:T(8,128)(2,1)S(1)}, bf16[96,3328]{1,0:T(8,128)(2,1)}, u32[]{:S(2)}, u32[]{:S(2)}) collective-permute-start(bf16[96,3328]{1,0:T(8,128)(2,1)S(1)} %get-tuple-element.60.own), channel_id=1, source_target_pairs={{0,1},{1,2},{2,3},{3,4},{4,5},{5,6},{6,7},{7,0},{8,9},{9,10},{10,1... | collective-permute-start | bytes 1916936 | tf_op jit(solution)/shard_map/ppermute | solution.py:23
  7.9 32.2 %collective-permute-start = (bf16[96,3328]{1,0:T(8,128)(2,1)S(1)}, bf16[96,3328]{1,0:T(8,128)(2,1)S(1)}, u32[]{:S(2)}, u32[]{:S(2)}) collective-permute-start(bf16[96,3328]{1,0:T(8,128)(2,1)S(1)} %get-tuple-element.61.own), channel_id=1, source_target_pairs={{0,1},{1,2},{2,3},{3,4},{4,5},{5,6},{6,7},{7,0},{8,9},{9,10},{10,1... | collective-permute-start | bytes 1916936 | tf_op jit(solution)/shard_map/ppermute | solution.py:23
  7.9 32.2 %collective-permute-start.3 = (bf16[96,3328]{1,0:T(8,128)(2,1)S(1)}, bf16[96,3328]{1,0:T(8,128)(2,1)S(1)}, u32[]{:S(2)}, u32[]{:S(2)}) collective-permute-start(bf16[96,3328]{1,0:T(8,128)(2,1)S(1)} %get-tuple-element.61.own), channel_id=1, source_target_pairs={{0,7},{1,0},{2,1},{3,2},{4,3},{5,4},{6,5},{7,6},{8,15},{9,8},{10,9... | collective-permute-start | bytes 1916936 | tf_op jit(solution)/shard_map/ppermute | solution.py:23
  11.9 14.6 %all-to-all-start = ((bf16[32,24,128]{2,1,0:T(8,128)(2,1)}), bf16[32,24,128]{2,1,0:T(8,128)(2,1)S(1)}, u32[]{:S(2)}, u32[]{:S(2)}) async-start(bf16[32,24,128]{2,1,0:T(8,128)(2,1)} %broadcast_in_dim.3), calls=%async_computation | async-start | bytes 393216 | tf_op jit(solution)/shard_map/all_to_all | solution.py:29
  22.7 27.4 %collective-permute-start.10 = (bf16[96,3328]{1,0:T(8,128)(2,1)S(1)}, bf16[96,3328]{1,0:T(8,128)(2,1)}, u32[]{:S(2)}, u32[]{:S(2)}) collective-permute-start(bf16[96,3328]{1,0:T(8,128)(2,1)S(1)} %collective-permute-done.9.l1), channel_id=1, source_target_pairs={{0,7},{1,0},{2,1},{3,2},{4,3},{5,4},{6,5},{7,6},{8,15},{9,8},{10,9... | collective-permute-start | bytes 1916936 | tf_op jit(solution)/shard_map/ppermute | solution.py:23
  26.5 27.4 %collective-permute-start.7 = (bf16[96,3328]{1,0:T(8,128)(2,1)}, bf16[96,3328]{1,0:T(8,128)(2,1)}, u32[]{:S(2)}, u32[]{:S(2)}) collective-permute-start(bf16[96,3328]{1,0:T(8,128)(2,1)} %collective-permute-done.6.r1), channel_id=1, source_target_pairs={{0,1},{1,2},{2,3},{3,4},{4,5},{5,6},{6,7},{7,0},{8,9},{9,10},{10,1... | collective-permute-start | bytes 1916936 | tf_op jit(solution)/shard_map/ppermute | solution.py:23
  40.1 23.7 %collective-permute-start.4 = (bf16[96,3328]{1,0:T(8,128)(2,1)S(1)}, bf16[96,3328]{1,0:T(8,128)(2,1)S(1)}, u32[]{:S(2)}, u32[]{:S(2)}) collective-permute-start(bf16[96,3328]{1,0:T(8,128)(2,1)S(1)} %collective-permute-done.3.l1), channel_id=1, source_target_pairs={{0,7},{1,0},{2,1},{3,2},{4,3},{5,4},{6,5},{7,6},{8,15},{9,8},{10,9... | collective-permute-start | bytes 1916936 | tf_op jit(solution)/shard_map/ppermute | solution.py:23
  40.1 27.4 %collective-permute-start.1 = (bf16[96,3328]{1,0:T(8,128)(2,1)S(1)}, bf16[96,3328]{1,0:T(8,128)(2,1)S(1)}, u32[]{:S(2)}, u32[]{:S(2)}) collective-permute-start(bf16[96,3328]{1,0:T(8,128)(2,1)S(1)} %collective-permute-done.r1), channel_id=1, source_target_pairs={{0,1},{1,2},{2,3},{3,4},{4,5},{5,6},{6,7},{7,0},{8,9},{9,10},{10,1... | collective-permute-start | bytes 1916936 | tf_op jit(solution)/shard_map/ppermute | solution.py:23
  50.1 27.5 %collective-permute-start.11 = (bf16[96,3328]{1,0:T(8,128)(2,1)}, bf16[96,3328]{1,0:T(8,128)(2,1)S(1)}, u32[]{:S(2)}, u32[]{:S(2)}) collective-permute-start(bf16[96,3328]{1,0:T(8,128)(2,1)} %collective-permute-done.10.l2), channel_id=1, source_target_pairs={{0,7},{1,0},{2,1},{3,2},{4,3},{5,4},{6,5},{7,6},{8,15},{9,8},{10,9... | collective-permute-start | bytes 1916936 | tf_op jit(solution)/shard_map/ppermute | solution.py:23
  53.9 27.4 %collective-permute-start.8 = (bf16[96,3328]{1,0:T(8,128)(2,1)}, bf16[96,3328]{1,0:T(8,128)(2,1)S(1)}, u32[]{:S(2)}, u32[]{:S(2)}) collective-permute-start(bf16[96,3328]{1,0:T(8,128)(2,1)} %collective-permute-done.7.r2), channel_id=1, source_target_pairs={{0,1},{1,2},{2,3},{3,4},{4,5},{5,6},{6,7},{7,0},{8,9},{9,10},{10,1... | collective-permute-start | bytes 1916936 | tf_op jit(solution)/shard_map/ppermute | solution.py:23
  63.8 27.4 %collective-permute-start.5 = (bf16[96,3328]{1,0:T(8,128)(2,1)S(1)}, bf16[96,3328]{1,0:T(8,128)(2,1)S(1)}, u32[]{:S(2)}, u32[]{:S(2)}) collective-permute-start(bf16[96,3328]{1,0:T(8,128)(2,1)S(1)} %collective-permute-done.4.l2), channel_id=1, source_target_pairs={{0,7},{1,0},{2,1},{3,2},{4,3},{5,4},{6,5},{7,6},{8,15},{9,8},{10,9... | collective-permute-start | bytes 1916936 | tf_op jit(solution)/shard_map/ppermute | solution.py:23
  67.5 27.4 %collective-permute-start.2 = (bf16[96,3328]{1,0:T(8,128)(2,1)S(1)}, bf16[96,3328]{1,0:T(8,128)(2,1)S(1)}, u32[]{:S(2)}, u32[]{:S(2)}) collective-permute-start(bf16[96,3328]{1,0:T(8,128)(2,1)S(1)} %collective-permute-done.1.r2), channel_id=1, source_target_pairs={{0,1},{1,2},{2,3},{3,4},{4,5},{5,6},{6,7},{7,0},{8,9},{9,10},{10,1... | collective-permute-start | bytes 1916936 | tf_op jit(solution)/shard_map/ppermute | solution.py:23
  77.6 21.9 %collective-permute-start.15 = (bf16[48,3328]{1,0:T(8,128)(2,1)S(1)}, bf16[48,3328]{1,0:T(8,128)(2,1)S(1)}, u32[]{:S(2)}, u32[]{:S(2)}) collective-permute-start(bf16[48,3328]{1,0:T(8,128)(2,1)S(1)} %half_of.7), channel_id=1, source_target_pairs={{0,7},{1,0},{2,1},{3,2},{4,3},{5,4},{6,5},{7,6},{8,15},{9,8},{10,9... | collective-permute-start | bytes 958472 | tf_op jit(solution)/shard_map/ppermute | solution.py:23
  81.3 20.4 %collective-permute-start.14 = (bf16[48,3328]{1,0:T(8,128)(2,1)S(1)}, bf16[48,3328]{1,0:T(8,128)(2,1)S(1)}, u32[]{:S(2)}, u32[]{:S(2)}) collective-permute-start(bf16[48,3328]{1,0:T(8,128)(2,1)S(1)} %half_of.6), channel_id=1, source_target_pairs={{0,1},{1,2},{2,3},{3,4},{4,5},{5,6},{6,7},{7,0},{8,9},{9,10},{10,1... | collective-permute-start | bytes 958472 | tf_op jit(solution)/shard_map/ppermute | solution.py:23
  94.9 6.8 %copy-start = (bf16[6656,128]{1,0:T(8,128)(2,1)S(1)}, bf16[6656,128]{1,0:T(8,128)(2,1)}, u32[]{:S(2)}) copy-start(bf16[6656,128]{1,0:T(8,128)(2,1)} %refs_5_.3) | copy-start | bytes 5111812
  94.9 11.5 %collective-permute-start.13 = (bf16[48,3328]{1,0:T(8,128)(2,1)S(1)}, bf16[48,3328]{1,0:T(8,128)(2,1)S(1)}, u32[]{:S(2)}, u32[]{:S(2)}) collective-permute-start(bf16[48,3328]{1,0:T(8,128)(2,1)S(1)} %half_of.5), channel_id=1, source_target_pairs={{0,7},{1,0},{2,1},{3,2},{4,3},{5,4},{6,5},{7,6},{8,15},{9,8},{10,9... | collective-permute-start | bytes 958472 | tf_op jit(solution)/shard_map/ppermute | solution.py:23
  95.0 12.1 %collective-permute-start.12 = (bf16[48,3328]{1,0:T(8,128)(2,1)S(1)}, bf16[48,3328]{1,0:T(8,128)(2,1)S(1)}, u32[]{:S(2)}, u32[]{:S(2)}) collective-permute-start(bf16[48,3328]{1,0:T(8,128)(2,1)S(1)} %half_of.4), channel_id=1, source_target_pairs={{0,1},{1,2},{2,3},{3,4},{4,5},{5,6},{6,7},{7,0},{8,9},{9,10},{10,1... | collective-permute-start | bytes 958472 | tf_op jit(solution)/shard_map/ppermute | solution.py:23
  111.9 22.7 %copy-start.1 = (f32[1024]{0:T(1024)S(1)}, f32[1024]{0:T(1024)}, u32[]{:S(2)}) copy-start(f32[1024]{0:T(1024)} %param.6) | copy-start | bytes 12292
  112.1 1.9 %collective-permute-start.16 = (f32[880,128]{1,0:T(8,128)S(1)}, f32[880,128]{1,0:T(8,128)S(1)}, u32[]{:S(2)}, u32[]{:S(2)}) collective-permute-start(f32[880,128]{1,0:T(8,128)S(1)} %get-tuple-element.49), channel_id=1, source_target_pairs={{0,8},{8,0},{1,9},{9,1},{2,10},{10,2},{3,11},{11,3},{4,12},{12,4},... | collective-permute-start | bytes 1351688 | tf_op jit(solution)/shard_map/ppermute | solution.py:23
  114.0 7.4 %collective-permute-start.17 = (f32[304,128]{1,0:T(8,128)S(1)}, f32[304,128]{1,0:T(8,128)S(1)}, u32[]{:S(2)}, u32[]{:S(2)}) collective-permute-start(f32[304,128]{1,0:T(8,128)S(1)} %get-tuple-element.51), channel_id=1, source_target_pairs={{0,64},{64,128},{128,192},{192,0},{1,65},{65,129},{129,193},{193,1... | collective-permute-start | bytes 466952 | tf_op jit(solution)/shard_map/ppermute | solution.py:23
  115.7 10.3 %collective-permute-start.18 = (f32[304,128]{1,0:T(8,128)S(1)}, f32[304,128]{1,0:T(8,128)S(1)}, u32[]{:S(2)}, u32[]{:S(2)}) collective-permute-start(f32[304,128]{1,0:T(8,128)S(1)} %get-tuple-element.52), channel_id=1, source_target_pairs={{0,128},{64,192},{128,0},{192,64},{1,129},{65,193},{129,1},{193,65... | collective-permute-start | bytes 466952 | tf_op jit(solution)/shard_map/ppermute | solution.py:23
  118.6 7.4 %collective-permute-start.19 = (f32[304,128]{1,0:T(8,128)S(1)}, f32[304,128]{1,0:T(8,128)S(1)}, u32[]{:S(2)}, u32[]{:S(2)}) collective-permute-start(f32[304,128]{1,0:T(8,128)S(1)} %get-tuple-element.53), channel_id=1, source_target_pairs={{0,192},{64,0},{128,64},{192,128},{1,193},{65,1},{129,65},{193,129... | collective-permute-start | bytes 466952 | tf_op jit(solution)/shard_map/ppermute | solution.py:23
  126.0 4.6 %collective-permute-start.20 = (f32[160,128]{1,0:T(8,128)S(1)}, f32[160,128]{1,0:T(8,128)S(1)}, u32[]{:S(2)}, u32[]{:S(2)}) collective-permute-start(f32[160,128]{1,0:T(8,128)S(1)} %get-tuple-element.55), channel_id=1, source_target_pairs={{0,16},{16,32},{32,48},{48,0},{1,17},{17,33},{33,49},{49,1},{2,18}... | collective-permute-start | bytes 245768 | tf_op jit(solution)/shard_map/ppermute | solution.py:23
  126.5 6.7 %collective-permute-start.21 = (f32[160,128]{1,0:T(8,128)S(1)}, f32[160,128]{1,0:T(8,128)S(1)}, u32[]{:S(2)}, u32[]{:S(2)}) collective-permute-start(f32[160,128]{1,0:T(8,128)S(1)} %get-tuple-element.56), channel_id=1, source_target_pairs={{0,32},{16,48},{32,0},{48,16},{1,33},{17,49},{33,1},{49,17},{2,34}... | collective-permute-start | bytes 245768 | tf_op jit(solution)/shard_map/ppermute | solution.py:23
  129.0 5.7 %collective-permute-start.22 = (f32[160,128]{1,0:T(8,128)S(1)}, f32[160,128]{1,0:T(8,128)S(1)}, u32[]{:S(2)}, u32[]{:S(2)}) collective-permute-start(f32[160,128]{1,0:T(8,128)S(1)} %get-tuple-element.57), channel_id=1, source_target_pairs={{0,48},{16,0},{32,16},{48,32},{1,49},{17,1},{33,17},{49,33},{2,50}... | collective-permute-start | bytes 245768 | tf_op jit(solution)/shard_map/ppermute | solution.py:23

commit v2 on v1

--- a/solution.py
+++ b/solution.py
@@ -250,7 +250,8 @@
         core = lax.axis_index("dp_2")
         for ref, parity in ((keep, core), (send, 1 - core)):
             for block in range(16):
-                row = pl.multiple_of(block * 2 * share + parity * share, 8)
+                from_block = jnp.where(parity == 0, block, block % 4 * 4 + block // 4)
+                row = pl.multiple_of((from_block * 2 + parity) * share, 8)
                 for side in range(2):
                     to = (block * 2 + side) * share
                     ref[to : to + share, :] = ab[
@@ -293,12 +294,15 @@
     return small_call(kernel, (shape, shape), (ab, hg, sx), "core_stage")
 
 
-def axis_stage(axis, received, rows_out):
+def axis_stage(first, received, rows_out):
     rows_in, channels = received[0].shape
 
     def kernel(*refs):
         ins, outs = refs[: len(received)], refs[len(received) :]
-        here = lax.axis_index(axis)
+        core_zero = lax.axis_index("dp_2") == 0
+        here = jnp.where(
+            core_zero if first else ~core_zero, lax.axis_index("dp_0"), lax.axis_index("dp_1")
+        )
         shared = ins[0][rows_in - COMMON :, :]
         for ref in ins[1:]:
             shared = shared + ref[rows_in - COMMON :, :]
@@ -312,6 +316,17 @@
 
     shape = jax.ShapeDtypeStruct((rows_out + COMMON, channels), f32)
     return small_call(kernel, (shape,) * 4, received, "axis_stage")
+
+
+def crossed(value, first, by):
+    pairs = []
+    for y in range(4):
+        for x in range(4):
+            for core in range(2):
+                along_y = (core == 0) == first
+                to = ((y + by) % 4, x) if along_y else (y, (x + by) % 4)
+                pairs.append(((y * 4 + x) * 2 + core, (to[0] * 4 + to[1]) * 2 + core))
+    return lax.ppermute(value, DP, pairs)
 
 
 def split(value):
@@ -439,10 +454,10 @@
         [flipped[:, lo:hi] for lo, hi in zip(bounds, bounds[1:])], bounds, cotangent, embed_weight
     )
     keep, send = core_stage(totals)
-    keep, *send = axis_stage("dp_0", (keep, shifted(send, "dp_2", 1)), 192)
-    came = [shifted(s, "dp_0", i + 1) for i, s in enumerate(send)]
-    keep, *send = axis_stage("dp_1", (keep, *came), 48)
-    came = [shifted(s, "dp_1", i + 1) for i, s in enumerate(send)]
+    keep, *send = axis_stage(True, (keep, shifted(send, "dp_2", 1)), 192)
+    came = [crossed(s, True, i + 1) for i, s in enumerate(send)]
+    keep, *send = axis_stage(False, (keep, *came), 48)
+    came = [crossed(s, False, i + 1) for i, s in enumerate(send)]
     gain = channel_gain.reshape(-1, embed_weight.shape[1])
     weight_grad, gain_grad = last_stage((keep, *came), gain, total_tokens)
     return weight_grad, gain_grad.reshape(-1)

time: 138 us -> 136 us (0.986)
  waiting for transfers between devices: 70.5 us -> 68.4 us
    ppermute x23 -> x17, waiting for transfers between devices: 70.5 us -> 58.8 us  [shifted(): lax.ppermute(value, axis, [(i, (i + by) % size) for i in range(size)])]
    ppermute x0 -> x6, waiting for transfers between devices: none -> 9.53 us  [crossed(): return lax.ppermute(value, DP, pairs)]
    ppermute x0 -> x6, starting transfers between devices: none -> 8.88 us  [crossed(): return lax.ppermute(value, DP, pairs)]
    ppermute x23 -> x17, starting transfers between devices: 37.4 us -> 28.5 us  [shifted(): lax.ppermute(value, axis, [(i, (i + by) % size) for i in range(size)])]
  transfers between devices with their start and end apart: 24 -> 24, of which waited for: 16 -> 17; matrix products, arithmetic and copies ran while one was open for 1% -> 1% of each run, Pallas kernels for 8% -> 8%
where the time goes in v2:
time: 136 us
  waiting for transfers between devices  68.4 us (50%)
  starting transfers between devices  45 us (33%)
  Pallas kernels  19.5 us (14%)
  local copies, waits for them, and re-layouts  2.09 us (2%)
    ppermute x17, waiting for transfers between devices, shifted(): lax.ppermute(value, axis, [(i, (i + by) % size) for i in range(size)])  58.8 us
    ppermute x17, starting transfers between devices, shifted(): lax.ppermute(value, axis, [(i, (i + by) % size) for i in range(size)])  28.5 us
    ppermute x6, waiting for transfers between devices, crossed(): return lax.ppermute(value, DP, pairs)  9.53 us
    pallas_call x2, Pallas kernels, far_step(): pl.pallas_call(kernel, out_shape=(jax.ShapeDtypeStruct(laid[0].shape, bf1...  9.45 us
    ppermute x6, starting transfers between devices, crossed(): return lax.ppermute(value, DP, pairs)  8.88 us
    all_to_all x1, starting transfers between devices, gathered_weights(): parts = lax.all_to_all(copies, DP, split_axis=0, concat_axis=0, tiled=True)  7.56 us
    pallas_call x2, Pallas kernels, near_step(): pl.pallas_call(kernel, out_shape=(jax.ShapeDtypeStruct((TILES, rows + cha...  6.47 us
    pallas_call x8, Pallas kernels, small_call(): pl.pallas_call(kernel, out_shape=outs, in_specs=[VMEM] * len(operands), o...  3.57 us
  transfers between devices with their start and end apart: 24, of which 17 were waited for; matrix products, arithmetic and copies ran while one was open for 1% of the time, Pallas kernels for 8%

profile of v2, /device:TPU:6, one launch (start us, length us, event | category | flops | bytes accessed | tf_op | source)
XLA Modules:
  0.0 135.7 jit_solution(4755364386960353793)
XLA Ops:
  0.6 1.4 %fusion = (bf16[96,3328]{1,0:T(8,128)(2,1)S(1)}, bf16[96,3328]{1,0:T(8,128)(2,1)S(1)}) fusion(bf16[96,6656]{1,0:T(8,128)(2,1)} %bitcast.9), kind=kLoop, calls=%fused_computation | loop fusion | bytes 2555904 | tf_op jit(solution)/shard_map/slice | solution.py:454
  2.0 5.9 %collective-permute-start.9 = (bf16[96,3328]{1,0:T(8,128)(2,1)S(1)}, bf16[96,3328]{1,0:T(8,128)(2,1)S(1)}, u32[]{:S(2)}, u32[]{:S(2)}) collective-permute-start(bf16[96,3328]{1,0:T(8,128)(2,1)S(1)} %get-tuple-element.60.own), channel_id=1, source_target_pairs={{0,7},{1,0},{2,1},{3,2},{4,3},{5,4},{6,5},{7,6},{8,15},{9,8},{10,9... | collective-permute-start | bytes 1916936 | tf_op jit(solution)/shard_map/ppermute | solution.py:23
  7.9 3.3 %collective-permute-start.3 = (bf16[96,3328]{1,0:T(8,128)(2,1)S(1)}, bf16[96,3328]{1,0:T(8,128)(2,1)S(1)}, u32[]{:S(2)}, u32[]{:S(2)}) collective-permute-start(bf16[96,3328]{1,0:T(8,128)(2,1)S(1)} %get-tuple-element.61.own), channel_id=1, source_target_pairs={{0,7},{1,0},{2,1},{3,2},{4,3},{5,4},{6,5},{7,6},{8,15},{9,8},{10,9... | collective-permute-start | bytes 1916936 | tf_op jit(solution)/shard_map/ppermute | solution.py:23
  11.2 0.7 broadcast_in_dim.3
  11.9 7.6 %all-to-all-start = ((bf16[32,24,128]{2,1,0:T(8,128)(2,1)}), bf16[32,24,128]{2,1,0:T(8,128)(2,1)S(1)}, u32[]{:S(2)}, u32[]{:S(2)}) async-start(bf16[32,24,128]{2,1,0:T(8,128)(2,1)} %broadcast_in_dim.3), calls=%async_computation | async-start | bytes 393216 | tf_op jit(solution)/shard_map/all_to_all | solution.py:29
  19.5 3.2 %collective-permute-done.9.l1 = bf16[96,3328]{1,0:T(8,128)(2,1)S(1)} collective-permute-done((bf16[96,3328]{1,0:T(8,128)(2,1)S(1)}, bf16[96,3328]{1,0:T(8,128)(2,1)S(1)}, u32[]{:S(2)}, u32[]{:S(2)}) %collective-permute-start.9) | collective-permute-done | bytes 639008 | tf_op jit(solution)/shard_map/ppermute | solution.py:23
  22.7 3.7 %collective-permute-start.10 = (bf16[96,3328]{1,0:T(8,128)(2,1)S(1)}, bf16[96,3328]{1,0:T(8,128)(2,1)}, u32[]{:S(2)}, u32[]{:S(2)}) collective-permute-start(bf16[96,3328]{1,0:T(8,128)(2,1)S(1)} %collective-permute-done.9.l1), channel_id=1, source_target_pairs={{0,7},{1,0},{2,1},{3,2},{4,3},{5,4},{6,5},{7,6},{8,15},{9,8},{10,9... | collective-permute-start | bytes 1916936 | tf_op jit(solution)/shard_map/ppermute | solution.py:23
  26.4 0.1 collective-permute-done.6.r1
  26.5 0.0 collective-permute-start.7
  26.5 0.0 all-to-all-done
  26.5 13.6 %collective-permute-done.r1 = bf16[96,3328]{1,0:T(8,128)(2,1)S(1)} collective-permute-done((bf16[96,3328]{1,0:T(8,128)(2,1)S(1)}, bf16[96,3328]{1,0:T(8,128)(2,1)S(1)}, u32[]{:S(2)}, u32[]{:S(2)}) %collective-permute-start) | collective-permute-done | bytes 639008 | tf_op jit(solution)/shard_map/ppermute | solution.py:23
  40.1 2.0 %collective-permute-start.1 = (bf16[96,3328]{1,0:T(8,128)(2,1)S(1)}, bf16[96,3328]{1,0:T(8,128)(2,1)S(1)}, u32[]{:S(2)}, u32[]{:S(2)}) collective-permute-start(bf16[96,3328]{1,0:T(8,128)(2,1)S(1)} %collective-permute-done.r1), channel_id=1, source_target_pairs={{0,1},{1,2},{2,3},{3,4},{4,5},{5,6},{6,7},{7,0},{8,9},{9,10},{10,1... | collective-permute-start | bytes 1916936 | tf_op jit(solution)/shard_map/ppermute | solution.py:23
  42.1 8.0 %collective-permute-done.10.l2 = bf16[96,3328]{1,0:T(8,128)(2,1)} collective-permute-done((bf16[96,3328]{1,0:T(8,128)(2,1)S(1)}, bf16[96,3328]{1,0:T(8,128)(2,1)}, u32[]{:S(2)}, u32[]{:S(2)}) %collective-permute-start.10) | collective-permute-done | bytes 639008 | tf_op jit(solution)/shard_map/ppermute | solution.py:23
  50.1 3.8 %collective-permute-start.11 = (bf16[96,3328]{1,0:T(8,128)(2,1)}, bf16[96,3328]{1,0:T(8,128)(2,1)S(1)}, u32[]{:S(2)}, u32[]{:S(2)}) collective-permute-start(bf16[96,3328]{1,0:T(8,128)(2,1)} %collective-permute-done.10.l2), channel_id=1, source_target_pairs={{0,7},{1,0},{2,1},{3,2},{4,3},{5,4},{6,5},{7,6},{8,15},{9,8},{10,9... | collective-permute-start | bytes 1916936 | tf_op jit(solution)/shard_map/ppermute | solution.py:23
  53.9 0.0 collective-permute-done.7.r2
  53.9 9.9 %collective-permute-done.4.l2 = bf16[96,3328]{1,0:T(8,128)(2,1)S(1)} collective-permute-done((bf16[96,3328]{1,0:T(8,128)(2,1)S(1)}, bf16[96,3328]{1,0:T(8,128)(2,1)S(1)}, u32[]{:S(2)}, u32[]{:S(2)}) %collective-permute-start.4) | collective-permute-done | bytes 639008 | tf_op jit(solution)/shard_map/ppermute | solution.py:23
  63.8 3.7 %collective-permute-start.5 = (bf16[96,3328]{1,0:T(8,128)(2,1)S(1)}, bf16[96,3328]{1,0:T(8,128)(2,1)S(1)}, u32[]{:S(2)}, u32[]{:S(2)}) collective-permute-start(bf16[96,3328]{1,0:T(8,128)(2,1)S(1)} %collective-permute-done.4.l2), channel_id=1, source_target_pairs={{0,7},{1,0},{2,1},{3,2},{4,3},{5,4},{6,5},{7,6},{8,15},{9,8},{10,9... | collective-permute-start | bytes 1916936 | tf_op jit(solution)/shard_map/ppermute | solution.py:23
  67.5 10.1 %collective-permute-done.11.l3.ref = bf16[96,3328]{1,0:T(8,128)(2,1)S(1)} collective-permute-done((bf16[96,3328]{1,0:T(8,128)(2,1)}, bf16[96,3328]{1,0:T(8,128)(2,1)S(1)}, u32[]{:S(2)}, u32[]{:S(2)}) %collective-permute-start.11) | collective-permute-done | bytes 639008 | tf_op jit(solution)/shard_map/ppermute | solution.py:23
  77.6 3.7 %collective-permute-start.15 = (bf16[48,3328]{1,0:T(8,128)(2,1)S(1)}, bf16[48,3328]{1,0:T(8,128)(2,1)S(1)}, u32[]{:S(2)}, u32[]{:S(2)}) collective-permute-start(bf16[48,3328]{1,0:T(8,128)(2,1)S(1)} %half_of.7), channel_id=1, source_target_pairs={{0,7},{1,0},{2,1},{3,2},{4,3},{5,4},{6,5},{7,6},{8,15},{9,8},{10,9... | collective-permute-start | bytes 958472 | tf_op jit(solution)/shard_map/ppermute | solution.py:23
  81.3 0.3 collective-permute-start.14
  81.6 4.0 %near.2 = (bf16[2,912,1664]{2,1,0:T(8,128)(2,1)S(1)}, f32[2,128,1664]{2,1,0:T(8,128)S(1)}, f32[768,128]{1,0:T(8,128)S(1)}) custom-call(bf16[96,3328]{1,0:T(8,128)(2,1)S(1)} %get-tuple-element.60.own, bf16[96,3328]{1,0:T(8,128)(2,1)} %collective-permute-done.6.r1, bf16[96,3328]{1,0:T(8,128)(2,1)} %collective-permute-done.7.r2, ...), custom_call_target="tpu_custom_call" | custom-call | flops 654311424 | bytes 5111808 | tf_op jit(solution)/shard_map/near/pallas_call | solution.py:117
  85.6 5.6 %collective-permute-done.5.ref.l3 = bf16[96,3328]{1,0:T(8,128)(2,1)S(1)} collective-permute-done((bf16[96,3328]{1,0:T(8,128)(2,1)S(1)}, bf16[96,3328]{1,0:T(8,128)(2,1)S(1)}, u32[]{:S(2)}, u32[]{:S(2)}) %collective-permute-start.5) | collective-permute-done | bytes 639008 | tf_op jit(solution)/shard_map/ppermute | solution.py:23
  91.2 3.7 %collective-permute-done.2.ref.r3 = bf16[96,3328]{1,0:T(8,128)(2,1)S(1)} collective-permute-done((bf16[96,3328]{1,0:T(8,128)(2,1)S(1)}, bf16[96,3328]{1,0:T(8,128)(2,1)S(1)}, u32[]{:S(2)}, u32[]{:S(2)}) %collective-permute-start.2) | collective-permute-done | bytes 639008 | tf_op jit(solution)/shard_map/ppermute | solution.py:23
  94.9 0.0 copy-start
  94.9 0.1 collective-permute-start.13
  95.0 2.0 %collective-permute-start.12 = (bf16[48,3328]{1,0:T(8,128)(2,1)S(1)}, bf16[48,3328]{1,0:T(8,128)(2,1)S(1)}, u32[]{:S(2)}, u32[]{:S(2)}) collective-permute-start(bf16[48,3328]{1,0:T(8,128)(2,1)S(1)} %half_of.4), channel_id=1, source_target_pairs={{0,1},{1,2},{2,3},{3,4},{4,5},{5,6},{6,7},{7,0},{8,9},{9,10},{10,1... | collective-permute-start | bytes 958472 | tf_op jit(solution)/shard_map/ppermute | solution.py:23
  97.0 2.5 %near.3 = (bf16[2,912,1664]{2,1,0:T(8,128)(2,1)S(1)}, f32[2,128,1664]{2,1,0:T(8,128)S(1)}, f32[768,128]{1,0:T(8,128)S(1)}) custom-call(bf16[96,3328]{1,0:T(8,128)(2,1)S(1)} %get-tuple-element.61.own, bf16[96,3328]{1,0:T(8,128)(2,1)S(1)} %collective-permute-done.r1, bf16[96,3328]{1,0:T(8,128)(2,1)S(1)} %collective-permute-done.1.r2, ...), custom_call_target="tpu_custom_call" | custom-call | flops 654311424 | bytes 5111808 | tf_op jit(solution)/shard_map/near/pallas_call | solution.py:117
  99.6 2.2 %collective-permute-done.14.refs_0_ = bf16[48,3328]{1,0:T(8,128)(2,1)S(1)} collective-permute-done((bf16[48,3328]{1,0:T(8,128)(2,1)S(1)}, bf16[48,3328]{1,0:T(8,128)(2,1)S(1)}, u32[]{:S(2)}, u32[]{:S(2)}) %collective-permute-start.14) | collective-permute-done | bytes 319520 | tf_op jit(solution)/shard_map/ppermute | solution.py:23
  101.7 4.7 %far.2 = (bf16[2,912,1664]{2,1,0:T(8,128)(2,1)S(1)}, f32[768,256]{1,0:T(8,128)S(1)}, f32[136,256]{1,0:T(8,128)S(1)}, f32[768,128]{1,0:T(8,128)S(1)}) custom-call(bf16[48,3328]{1,0:T(8,128)(2,1)S(1)} %collective-permute-done.14.refs_0_, bf16[48,3328]{1,0:T(8,128)(2,1)S(1)} %collective-permute-done.15.refs_1_, ...), custom_call_target="tpu_custom_call", output_to_operand_aliasing={{0}: (2, {})} | custom-call | flops 1526726656 | bytes 5111808 | tf_op jit(solution)/shard_map/far/pallas_call | solution.py:203
  106.4 0.7 collective-permute-done.12.refs_0_
  107.1 4.7 %far.3 = (bf16[2,912,1664]{2,1,0:T(8,128)(2,1)S(1)}, f32[768,256]{1,0:T(8,128)S(1)}, f32[136,256]{1,0:T(8,128)S(1)}, f32[768,128]{1,0:T(8,128)S(1)}) custom-call(bf16[48,3328]{1,0:T(8,128)(2,1)S(1)} %collective-permute-done.12.refs_0_, ...), custom_call_target="tpu_custom_call", output_to_operand_aliasing={{0}: (2, {}), {1}: (7, {}), {2}: (8, {}), {3}: (9, {})} | custom-call | flops 1526726656 | bytes 5111808 | tf_op jit(solution)/shard_map/far/pallas_call | solution.py:203
  111.9 0.0 copy-start.1
  111.9 0.2 core_stage.1
  112.1 0.1 collective-permute-start.16
  112.2 1.8 %collective-permute-done.16.refs_1_ = f32[880,128]{1,0:T(8,128)S(1)} collective-permute-done((f32[880,128]{1,0:T(8,128)S(1)}, f32[880,128]{1,0:T(8,128)S(1)}, u32[]{:S(2)}, u32[]{:S(2)}) %collective-permute-start.16) | collective-permute-done | bytes 450592 | tf_op jit(solution)/shard_map/ppermute | solution.py:23
  114.0 0.1 axis_stage.2
  114.0 1.7 %collective-permute-start.17 = (f32[304,128]{1,0:T(8,128)S(1)}, f32[304,128]{1,0:T(8,128)S(1)}, u32[]{:S(2)}, u32[]{:S(2)}) collective-permute-start(f32[304,128]{1,0:T(8,128)S(1)} %get-tuple-element.51), channel_id=1, source_target_pairs={{0,64},{8,24},{16,80},{24,40},{32,96},{40,56},{48,112},{56,8},{64,... | collective-permute-start | bytes 466952 | tf_op jit(solution)/shard_map/ppermute | solution.py:329
  115.7 2.9 %collective-permute-start.18 = (f32[304,128]{1,0:T(8,128)S(1)}, f32[304,128]{1,0:T(8,128)S(1)}, u32[]{:S(2)}, u32[]{:S(2)}) collective-permute-start(f32[304,128]{1,0:T(8,128)S(1)} %get-tuple-element.52), channel_id=1, source_target_pairs={{0,128},{8,40},{16,144},{24,56},{32,160},{40,8},{48,176},{56,24},{... | collective-permute-start | bytes 466952 | tf_op jit(solution)/shard_map/ppermute | solution.py:329
  118.6 1.3 collective-permute-start.19
  119.9 0.6 collective-permute-done.17.refs_1_
  120.5 2.9 %collective-permute-done.18.refs_2_ = f32[304,128]{1,0:T(8,128)S(1)} collective-permute-done((f32[304,128]{1,0:T(8,128)S(1)}, f32[304,128]{1,0:T(8,128)S(1)}, u32[]{:S(2)}, u32[]{:S(2)}) %collective-permute-start.18) | collective-permute-done | bytes 155680 | tf_op jit(solution)/shard_map/ppermute | solution.py:329
  123.5 0.4 collective-permute-done.19.refs_3_
  123.9 0.6 collective-permute-start.20
  124.4 2.4 %collective-permute-start.21 = (f32[160,128]{1,0:T(8,128)S(1)}, f32[160,128]{1,0:T(8,128)S(1)}, u32[]{:S(2)}, u32[]{:S(2)}) collective-permute-start(f32[160,128]{1,0:T(8,128)S(1)} %get-tuple-element.56), channel_id=1, source_target_pairs={{0,32},{8,136},{16,48},{24,152},{32,0},{40,168},{48,16},{56,184},{... | collective-permute-start | bytes 245768 | tf_op jit(solution)/shard_map/ppermute | solution.py:329
  126.8 1.5 %collective-permute-done.20.refs_1_ = f32[160,128]{1,0:T(8,128)S(1)} collective-permute-done((f32[160,128]{1,0:T(8,128)S(1)}, f32[160,128]{1,0:T(8,128)S(1)}, u32[]{:S(2)}, u32[]{:S(2)}) %collective-permute-start.20) | collective-permute-done | bytes 81952 | tf_op jit(solution)/shard_map/ppermute | solution.py:329
  128.4 2.0 %collective-permute-done.21.refs_2_ = f32[160,128]{1,0:T(8,128)S(1)} collective-permute-done((f32[160,128]{1,0:T(8,128)S(1)}, f32[160,128]{1,0:T(8,128)S(1)}, u32[]{:S(2)}, u32[]{:S(2)}) %collective-permute-start.21) | collective-permute-done | bytes 81952 | tf_op jit(solution)/shard_map/ppermute | solution.py:329
  130.4 2.1 %collective-permute-done.22.refs_3_ = f32[160,128]{1,0:T(8,128)S(1)} collective-permute-done((f32[160,128]{1,0:T(8,128)S(1)}, f32[160,128]{1,0:T(8,128)S(1)}, u32[]{:S(2)}, u32[]{:S(2)}) %collective-permute-start.22) | collective-permute-done | bytes 81952 | tf_op jit(solution)/shard_map/ppermute | solution.py:329
  132.5 3.2 %last_stage.1 = (f32[24,128]{1,0:T(8,128)}, f32[1,128]{1,0:T(1,128)}) custom-call(f32[160,128]{1,0:T(8,128)S(1)} %get-tuple-element.54.refs_0_, f32[160,128]{1,0:T(8,128)S(1)} %collective-permute-done.20.refs_1_, f32[160,128]{1,0:T(8,128)S(1)} %collective-permute-done.21.refs_2_, f32[160,128]{1,0:T(8,128)S(1)} %collective-permute-done.22.refs_3_, ...), custom_call_target="tpu_custom_call" | custom-call | flops 1000000 | bytes 1000000 | tf_op jit(solution)/shard_map/last_stage/pallas_call | solution.py:230
  (20 shorter events, 0.2 us)
Async XLA Ops:
  0.6 10.6 %copy-start.2 = (bf16[24,128]{1,0:T(8,128)(2,1)S(1)}, bf16[24,128]{1,0:T(8,128)(2,1)}, u32[]{:S(2)}) copy-start(bf16[24,128]{1,0:T(8,128)(2,1)} %param.5) | copy-start | bytes 18436
  2.0 20.7 %collective-permute-start.9 = (bf16[96,3328]{1,0:T(8,128)(2,1)S(1)}, bf16[96,3328]{1,0:T(8,128)(2,1)S(1)}, u32[]{:S(2)}, u32[]{:S(2)}) collective-permute-start(bf16[96,3328]{1,0:T(8,128)(2,1)S(1)} %get-tuple-element.60.own), channel_id=1, source_target_pairs={{0,7},{1,0},{2,1},{3,2},{4,3},{5,4},{6,5},{7,6},{8,15},{9,8},{10,9... | collective-permute-start | bytes 1916936 | tf_op jit(solution)/shard_map/ppermute | solution.py:23
  7.9 18.6 %collective-permute-start.6 = (bf16[96,3328]{1,0:T(8,128)(2,1)S(1)}, bf16[96,3328]{1,0:T(8,128)(2,1)}, u32[]{:S(2)}, u32[]{:S(2)}) collective-permute-start(bf16[96,3328]{1,0:T(8,128)(2,1)S(1)} %get-tuple-element.60.own), channel_id=1, source_target_pairs={{0,1},{1,2},{2,3},{3,4},{4,5},{5,6},{6,7},{7,0},{8,9},{9,10},{10,1... | collective-permute-start | bytes 1916936 | tf_op jit(solution)/shard_map/ppermute | solution.py:23
  7.9 32.2 %collective-permute-start = (bf16[96,3328]{1,0:T(8,128)(2,1)S(1)}, bf16[96,3328]{1,0:T(8,128)(2,1)S(1)}, u32[]{:S(2)}, u32[]{:S(2)}) collective-permute-start(bf16[96,3328]{1,0:T(8,128)(2,1)S(1)} %get-tuple-element.61.own), channel_id=1, source_target_pairs={{0,1},{1,2},{2,3},{3,4},{4,5},{5,6},{6,7},{7,0},{8,9},{9,10},{10,1... | collective-permute-start | bytes 1916936 | tf_op jit(solution)/shard_map/ppermute | solution.py:23
  7.9 32.2 %collective-permute-start.3 = (bf16[96,3328]{1,0:T(8,128)(2,1)S(1)}, bf16[96,3328]{1,0:T(8,128)(2,1)S(1)}, u32[]{:S(2)}, u32[]{:S(2)}) collective-permute-start(bf16[96,3328]{1,0:T(8,128)(2,1)S(1)} %get-tuple-element.61.own), channel_id=1, source_target_pairs={{0,7},{1,0},{2,1},{3,2},{4,3},{5,4},{6,5},{7,6},{8,15},{9,8},{10,9... | collective-permute-start | bytes 1916936 | tf_op jit(solution)/shard_map/ppermute | solution.py:23
  11.9 14.6 %all-to-all-start = ((bf16[32,24,128]{2,1,0:T(8,128)(2,1)}), bf16[32,24,128]{2,1,0:T(8,128)(2,1)S(1)}, u32[]{:S(2)}, u32[]{:S(2)}) async-start(bf16[32,24,128]{2,1,0:T(8,128)(2,1)} %broadcast_in_dim.3), calls=%async_computation | async-start | bytes 393216 | tf_op jit(solution)/shard_map/all_to_all | solution.py:29
  22.7 27.4 %collective-permute-start.10 = (bf16[96,3328]{1,0:T(8,128)(2,1)S(1)}, bf16[96,3328]{1,0:T(8,128)(2,1)}, u32[]{:S(2)}, u32[]{:S(2)}) collective-permute-start(bf16[96,3328]{1,0:T(8,128)(2,1)S(1)} %collective-permute-done.9.l1), channel_id=1, source_target_pairs={{0,7},{1,0},{2,1},{3,2},{4,3},{5,4},{6,5},{7,6},{8,15},{9,8},{10,9... | collective-permute-start | bytes 1916936 | tf_op jit(solution)/shard_map/ppermute | solution.py:23
  26.5 27.4 %collective-permute-start.7 = (bf16[96,3328]{1,0:T(8,128)(2,1)}, bf16[96,3328]{1,0:T(8,128)(2,1)}, u32[]{:S(2)}, u32[]{:S(2)}) collective-permute-start(bf16[96,3328]{1,0:T(8,128)(2,1)} %collective-permute-done.6.r1), channel_id=1, source_target_pairs={{0,1},{1,2},{2,3},{3,4},{4,5},{5,6},{6,7},{7,0},{8,9},{9,10},{10,1... | collective-permute-start | bytes 1916936 | tf_op jit(solution)/shard_map/ppermute | solution.py:23
  40.1 23.7 %collective-permute-start.4 = (bf16[96,3328]{1,0:T(8,128)(2,1)S(1)}, bf16[96,3328]{1,0:T(8,128)(2,1)S(1)}, u32[]{:S(2)}, u32[]{:S(2)}) collective-permute-start(bf16[96,3328]{1,0:T(8,128)(2,1)S(1)} %collective-permute-done.3.l1), channel_id=1, source_target_pairs={{0,7},{1,0},{2,1},{3,2},{4,3},{5,4},{6,5},{7,6},{8,15},{9,8},{10,9... | collective-permute-start | bytes 1916936 | tf_op jit(solution)/shard_map/ppermute | solution.py:23
  40.1 27.4 %collective-permute-start.1 = (bf16[96,3328]{1,0:T(8,128)(2,1)S(1)}, bf16[96,3328]{1,0:T(8,128)(2,1)S(1)}, u32[]{:S(2)}, u32[]{:S(2)}) collective-permute-start(bf16[96,3328]{1,0:T(8,128)(2,1)S(1)} %collective-permute-done.r1), channel_id=1, source_target_pairs={{0,1},{1,2},{2,3},{3,4},{4,5},{5,6},{6,7},{7,0},{8,9},{9,10},{10,1... | collective-permute-start | bytes 1916936 | tf_op jit(solution)/shard_map/ppermute | solution.py:23
  50.1 27.5 %collective-permute-start.11 = (bf16[96,3328]{1,0:T(8,128)(2,1)}, bf16[96,3328]{1,0:T(8,128)(2,1)S(1)}, u32[]{:S(2)}, u32[]{:S(2)}) collective-permute-start(bf16[96,3328]{1,0:T(8,128)(2,1)} %collective-permute-done.10.l2), channel_id=1, source_target_pairs={{0,7},{1,0},{2,1},{3,2},{4,3},{5,4},{6,5},{7,6},{8,15},{9,8},{10,9... | collective-permute-start | bytes 1916936 | tf_op jit(solution)/shard_map/ppermute | solution.py:23
  53.9 27.4 %collective-permute-start.8 = (bf16[96,3328]{1,0:T(8,128)(2,1)}, bf16[96,3328]{1,0:T(8,128)(2,1)S(1)}, u32[]{:S(2)}, u32[]{:S(2)}) collective-permute-start(bf16[96,3328]{1,0:T(8,128)(2,1)} %collective-permute-done.7.r2), channel_id=1, source_target_pairs={{0,1},{1,2},{2,3},{3,4},{4,5},{5,6},{6,7},{7,0},{8,9},{9,10},{10,1... | collective-permute-start | bytes 1916936 | tf_op jit(solution)/shard_map/ppermute | solution.py:23
  63.8 27.4 %collective-permute-start.5 = (bf16[96,3328]{1,0:T(8,128)(2,1)S(1)}, bf16[96,3328]{1,0:T(8,128)(2,1)S(1)}, u32[]{:S(2)}, u32[]{:S(2)}) collective-permute-start(bf16[96,3328]{1,0:T(8,128)(2,1)S(1)} %collective-permute-done.4.l2), channel_id=1, source_target_pairs={{0,7},{1,0},{2,1},{3,2},{4,3},{5,4},{6,5},{7,6},{8,15},{9,8},{10,9... | collective-permute-start | bytes 1916936 | tf_op jit(solution)/shard_map/ppermute | solution.py:23
  67.5 27.4 %collective-permute-start.2 = (bf16[96,3328]{1,0:T(8,128)(2,1)S(1)}, bf16[96,3328]{1,0:T(8,128)(2,1)S(1)}, u32[]{:S(2)}, u32[]{:S(2)}) collective-permute-start(bf16[96,3328]{1,0:T(8,128)(2,1)S(1)} %collective-permute-done.1.r2), channel_id=1, source_target_pairs={{0,1},{1,2},{2,3},{3,4},{4,5},{5,6},{6,7},{7,0},{8,9},{9,10},{10,1... | collective-permute-start | bytes 1916936 | tf_op jit(solution)/shard_map/ppermute | solution.py:23
  77.6 21.9 %collective-permute-start.15 = (bf16[48,3328]{1,0:T(8,128)(2,1)S(1)}, bf16[48,3328]{1,0:T(8,128)(2,1)S(1)}, u32[]{:S(2)}, u32[]{:S(2)}) collective-permute-start(bf16[48,3328]{1,0:T(8,128)(2,1)S(1)} %half_of.7), channel_id=1, source_target_pairs={{0,7},{1,0},{2,1},{3,2},{4,3},{5,4},{6,5},{7,6},{8,15},{9,8},{10,9... | collective-permute-start | bytes 958472 | tf_op jit(solution)/shard_map/ppermute | solution.py:23
  81.3 20.4 %collective-permute-start.14 = (bf16[48,3328]{1,0:T(8,128)(2,1)S(1)}, bf16[48,3328]{1,0:T(8,128)(2,1)S(1)}, u32[]{:S(2)}, u32[]{:S(2)}) collective-permute-start(bf16[48,3328]{1,0:T(8,128)(2,1)S(1)} %half_of.6), channel_id=1, source_target_pairs={{0,1},{1,2},{2,3},{3,4},{4,5},{5,6},{6,7},{7,0},{8,9},{9,10},{10,1... | collective-permute-start | bytes 958472 | tf_op jit(solution)/shard_map/ppermute | solution.py:23
  94.9 6.8 %copy-start = (bf16[6656,128]{1,0:T(8,128)(2,1)S(1)}, bf16[6656,128]{1,0:T(8,128)(2,1)}, u32[]{:S(2)}) copy-start(bf16[6656,128]{1,0:T(8,128)(2,1)} %refs_5_.3) | copy-start | bytes 5111812
  94.9 11.5 %collective-permute-start.13 = (bf16[48,3328]{1,0:T(8,128)(2,1)S(1)}, bf16[48,3328]{1,0:T(8,128)(2,1)S(1)}, u32[]{:S(2)}, u32[]{:S(2)}) collective-permute-start(bf16[48,3328]{1,0:T(8,128)(2,1)S(1)} %half_of.5), channel_id=1, source_target_pairs={{0,7},{1,0},{2,1},{3,2},{4,3},{5,4},{6,5},{7,6},{8,15},{9,8},{10,9... | collective-permute-start | bytes 958472 | tf_op jit(solution)/shard_map/ppermute | solution.py:23
  95.0 12.1 %collective-permute-start.12 = (bf16[48,3328]{1,0:T(8,128)(2,1)S(1)}, bf16[48,3328]{1,0:T(8,128)(2,1)S(1)}, u32[]{:S(2)}, u32[]{:S(2)}) collective-permute-start(bf16[48,3328]{1,0:T(8,128)(2,1)S(1)} %half_of.4), channel_id=1, source_target_pairs={{0,1},{1,2},{2,3},{3,4},{4,5},{5,6},{6,7},{7,0},{8,9},{9,10},{10,1... | collective-permute-start | bytes 958472 | tf_op jit(solution)/shard_map/ppermute | solution.py:23
  111.9 20.6 %copy-start.1 = (f32[1024]{0:T(1024)S(1)}, f32[1024]{0:T(1024)}, u32[]{:S(2)}) copy-start(f32[1024]{0:T(1024)} %param.6) | copy-start | bytes 12292
  112.1 1.9 %collective-permute-start.16 = (f32[880,128]{1,0:T(8,128)S(1)}, f32[880,128]{1,0:T(8,128)S(1)}, u32[]{:S(2)}, u32[]{:S(2)}) collective-permute-start(f32[880,128]{1,0:T(8,128)S(1)} %get-tuple-element.49), channel_id=1, source_target_pairs={{0,8},{8,0},{1,9},{9,1},{2,10},{10,2},{3,11},{11,3},{4,12},{12,4},... | collective-permute-start | bytes 1351688 | tf_op jit(solution)/shard_map/ppermute | solution.py:23
  114.0 6.5 %collective-permute-start.17 = (f32[304,128]{1,0:T(8,128)S(1)}, f32[304,128]{1,0:T(8,128)S(1)}, u32[]{:S(2)}, u32[]{:S(2)}) collective-permute-start(f32[304,128]{1,0:T(8,128)S(1)} %get-tuple-element.51), channel_id=1, source_target_pairs={{0,64},{8,24},{16,80},{24,40},{32,96},{40,56},{48,112},{56,8},{64,... | collective-permute-start | bytes 466952 | tf_op jit(solution)/shard_map/ppermute | solution.py:329
  115.7 7.8 %collective-permute-start.18 = (f32[304,128]{1,0:T(8,128)S(1)}, f32[304,128]{1,0:T(8,128)S(1)}, u32[]{:S(2)}, u32[]{:S(2)}) collective-permute-start(f32[304,128]{1,0:T(8,128)S(1)} %get-tuple-element.52), channel_id=1, source_target_pairs={{0,128},{8,40},{16,144},{24,56},{32,160},{40,8},{48,176},{56,24},{... | collective-permute-start | bytes 466952 | tf_op jit(solution)/shard_map/ppermute | solution.py:329
  118.6 5.2 %collective-permute-start.19 = (f32[304,128]{1,0:T(8,128)S(1)}, f32[304,128]{1,0:T(8,128)S(1)}, u32[]{:S(2)}, u32[]{:S(2)}) collective-permute-start(f32[304,128]{1,0:T(8,128)S(1)} %get-tuple-element.53), channel_id=1, source_target_pairs={{0,192},{8,56},{16,208},{24,8},{32,224},{40,24},{48,240},{56,40},{... | collective-permute-start | bytes 466952 | tf_op jit(solution)/shard_map/ppermute | solution.py:329
  123.9 4.5 %collective-permute-start.20 = (f32[160,128]{1,0:T(8,128)S(1)}, f32[160,128]{1,0:T(8,128)S(1)}, u32[]{:S(2)}, u32[]{:S(2)}) collective-permute-start(f32[160,128]{1,0:T(8,128)S(1)} %get-tuple-element.55), channel_id=1, source_target_pairs={{0,16},{8,72},{16,32},{24,88},{32,48},{40,104},{48,0},{56,120},{64... | collective-permute-start | bytes 245768 | tf_op jit(solution)/shard_map/ppermute | solution.py:329
  124.4 5.9 %collective-permute-start.21 = (f32[160,128]{1,0:T(8,128)S(1)}, f32[160,128]{1,0:T(8,128)S(1)}, u32[]{:S(2)}, u32[]{:S(2)}) collective-permute-start(f32[160,128]{1,0:T(8,128)S(1)} %get-tuple-element.56), channel_id=1, source_target_pairs={{0,32},{8,136},{16,48},{24,152},{32,0},{40,168},{48,16},{56,184},{... | collective-permute-start | bytes 245768 | tf_op jit(solution)/shard_map/ppermute | solution.py:329
  126.8 5.7 %collective-permute-start.22 = (f32[160,128]{1,0:T(8,128)S(1)}, f32[160,128]{1,0:T(8,128)S(1)}, u32[]{:S(2)}, u32[]{:S(2)}) collective-permute-start(f32[160,128]{1,0:T(8,128)S(1)} %get-tuple-element.57), channel_id=1, source_target_pairs={{0,48},{8,200},{16,0},{24,216},{32,16},{40,232},{48,32},{56,248},{... | collective-permute-start | bytes 245768 | tf_op jit(solution)/shard_map/ppermute | solution.py:329

commit v3 on v2

--- a/solution.py
+++ b/solution.py
@@ -180,9 +180,10 @@
         sums = near_sx[...] + ins[2][...] if accumulate else near_sx[...]
         sx[...] = sums
         sx[pl.ds(row, width), :] = sx[pl.ds(row, width), :] + far_sx
+        for step in moves:
+            for move in step:
+                move.wait()
         for step in range(TILES):
-            for move in moves[step]:
-                move.wait()
             et = near[step] + jnp.dot(
                 w_far, big[step, pl.ds(row, width), :], preferred_element_type=f32
             )
@@ -239,6 +240,7 @@
 
 
 COMMON = 112
+FAR_FIRST = (2, 1, 3)
 
 
 def core_stage(totals):
@@ -455,9 +457,9 @@
     )
     keep, send = core_stage(totals)
     keep, *send = axis_stage(True, (keep, shifted(send, "dp_2", 1)), 192)
-    came = [crossed(s, True, i + 1) for i, s in enumerate(send)]
+    came = [crossed(send[by - 1], True, by) for by in FAR_FIRST]
     keep, *send = axis_stage(False, (keep, *came), 48)
-    came = [crossed(s, False, i + 1) for i, s in enumerate(send)]
+    came = [crossed(send[by - 1], False, by) for by in FAR_FIRST]
     gain = channel_gain.reshape(-1, embed_weight.shape[1])
     weight_grad, gain_grad = last_stage((keep, *came), gain, total_tokens)
     return weight_grad, gain_grad.reshape(-1)

time: 136 us -> 137 us (level)
  transfers between devices with their start and end apart: 24 -> 24, of which waited for: 17 -> 15; matrix products, arithmetic and copies ran while one was open for 1% -> 1% of each run, Pallas kernels for 8% -> 8%
where the time goes in v3:
time: 137 us; the launch traced here: 136 us
  waiting for transfers between devices  67.9 us (50%)
  starting transfers between devices  46.2 us (34%)
  Pallas kernels  19.2 us (14%)
  local copies, waits for them, and re-layouts  2.09 us (2%)
    ppermute x17, waiting for transfers between devices, shifted(): lax.ppermute(value, axis, [(i, (i + by) % size) for i in range(size)])  59 us
    ppermute x17, starting transfers between devices, shifted(): lax.ppermute(value, axis, [(i, (i + by) % size) for i in range(size)])  28.5 us
    ppermute x6, starting transfers between devices, crossed(): return lax.ppermute(value, DP, pairs)  10.1 us
    pallas_call x2, Pallas kernels, far_step(): pl.pallas_call(kernel, out_shape=(jax.ShapeDtypeStruct(laid[0].shape, bf1...  9.15 us
    ppermute x6, waiting for transfers between devices, crossed(): return lax.ppermute(value, DP, pairs)  8.85 us
    all_to_all x1, starting transfers between devices, gathered_weights(): parts = lax.all_to_all(copies, DP, split_axis=0, concat_axis=0, tiled=True)  7.56 us
    pallas_call x2, Pallas kernels, near_step(): pl.pallas_call(kernel, out_shape=(jax.ShapeDtypeStruct((TILES, rows + cha...  6.47 us
    pallas_call x8, Pallas kernels, small_call(): pl.pallas_call(kernel, out_shape=outs, in_specs=[VMEM] * len(operands), o...  3.57 us
  transfers between devices with their start and end apart: 24, of which 15 were waited for; matrix products, arithmetic and copies ran while one was open for 1% of the time, Pallas kernels for 8%

profile of v3, /device:TPU:6, one launch (start us, length us, event | category | flops | bytes accessed | tf_op | source)
XLA Modules:
  0.0 136.1 jit_solution(5472808706043011188)
XLA Ops:
  0.6 1.4 %fusion = (bf16[96,3328]{1,0:T(8,128)(2,1)S(1)}, bf16[96,3328]{1,0:T(8,128)(2,1)S(1)}) fusion(bf16[96,6656]{1,0:T(8,128)(2,1)} %bitcast.9), kind=kLoop, calls=%fused_computation | loop fusion | bytes 2555904 | tf_op jit(solution)/shard_map/slice | solution.py:456
  2.0 5.9 %collective-permute-start.9 = (bf16[96,3328]{1,0:T(8,128)(2,1)S(1)}, bf16[96,3328]{1,0:T(8,128)(2,1)S(1)}, u32[]{:S(2)}, u32[]{:S(2)}) collective-permute-start(bf16[96,3328]{1,0:T(8,128)(2,1)S(1)} %get-tuple-element.60.own), channel_id=1, source_target_pairs={{0,7},{1,0},{2,1},{3,2},{4,3},{5,4},{6,5},{7,6},{8,15},{9,8},{10,9... | collective-permute-start | bytes 1916936 | tf_op jit(solution)/shard_map/ppermute | solution.py:23
  7.9 0.0 collective-permute-start.6
  7.9 3.3 %collective-permute-start.3 = (bf16[96,3328]{1,0:T(8,128)(2,1)S(1)}, bf16[96,3328]{1,0:T(8,128)(2,1)S(1)}, u32[]{:S(2)}, u32[]{:S(2)}) collective-permute-start(bf16[96,3328]{1,0:T(8,128)(2,1)S(1)} %get-tuple-element.61.own), channel_id=1, source_target_pairs={{0,7},{1,0},{2,1},{3,2},{4,3},{5,4},{6,5},{7,6},{8,15},{9,8},{10,9... | collective-permute-start | bytes 1916936 | tf_op jit(solution)/shard_map/ppermute | solution.py:23
  11.2 0.7 broadcast_in_dim.3
  11.9 7.6 %all-to-all-start = ((bf16[32,24,128]{2,1,0:T(8,128)(2,1)}), bf16[32,24,128]{2,1,0:T(8,128)(2,1)S(1)}, u32[]{:S(2)}, u32[]{:S(2)}) async-start(bf16[32,24,128]{2,1,0:T(8,128)(2,1)} %broadcast_in_dim.3), calls=%async_computation | async-start | bytes 393216 | tf_op jit(solution)/shard_map/all_to_all | solution.py:29
  19.5 3.2 %collective-permute-done.9.l1 = bf16[96,3328]{1,0:T(8,128)(2,1)S(1)} collective-permute-done((bf16[96,3328]{1,0:T(8,128)(2,1)S(1)}, bf16[96,3328]{1,0:T(8,128)(2,1)S(1)}, u32[]{:S(2)}, u32[]{:S(2)}) %collective-permute-start.9) | collective-permute-done | bytes 639008 | tf_op jit(solution)/shard_map/ppermute | solution.py:23
  22.7 3.7 %collective-permute-start.10 = (bf16[96,3328]{1,0:T(8,128)(2,1)S(1)}, bf16[96,3328]{1,0:T(8,128)(2,1)}, u32[]{:S(2)}, u32[]{:S(2)}) collective-permute-start(bf16[96,3328]{1,0:T(8,128)(2,1)S(1)} %collective-permute-done.9.l1), channel_id=1, source_target_pairs={{0,7},{1,0},{2,1},{3,2},{4,3},{5,4},{6,5},{7,6},{8,15},{9,8},{10,9... | collective-permute-start | bytes 1916936 | tf_op jit(solution)/shard_map/ppermute | solution.py:23
  26.4 0.1 collective-permute-done.6.r1
  26.5 0.0 collective-permute-start.7
  26.5 0.0 all-to-all-done
  26.5 13.6 %collective-permute-done.r1 = bf16[96,3328]{1,0:T(8,128)(2,1)S(1)} collective-permute-done((bf16[96,3328]{1,0:T(8,128)(2,1)S(1)}, bf16[96,3328]{1,0:T(8,128)(2,1)S(1)}, u32[]{:S(2)}, u32[]{:S(2)}) %collective-permute-start) | collective-permute-done | bytes 639008 | tf_op jit(solution)/shard_map/ppermute | solution.py:23
  40.1 0.0 collective-permute-done.3.l1
  40.1 0.0 collective-permute-start.4
  40.1 2.0 %collective-permute-start.1 = (bf16[96,3328]{1,0:T(8,128)(2,1)S(1)}, bf16[96,3328]{1,0:T(8,128)(2,1)S(1)}, u32[]{:S(2)}, u32[]{:S(2)}) collective-permute-start(bf16[96,3328]{1,0:T(8,128)(2,1)S(1)} %collective-permute-done.r1), channel_id=1, source_target_pairs={{0,1},{1,2},{2,3},{3,4},{4,5},{5,6},{6,7},{7,0},{8,9},{9,10},{10,1... | collective-permute-start | bytes 1916936 | tf_op jit(solution)/shard_map/ppermute | solution.py:23
  42.1 8.0 %collective-permute-done.10.l2 = bf16[96,3328]{1,0:T(8,128)(2,1)} collective-permute-done((bf16[96,3328]{1,0:T(8,128)(2,1)S(1)}, bf16[96,3328]{1,0:T(8,128)(2,1)}, u32[]{:S(2)}, u32[]{:S(2)}) %collective-permute-start.10) | collective-permute-done | bytes 639008 | tf_op jit(solution)/shard_map/ppermute | solution.py:23
  50.1 3.8 %collective-permute-start.11 = (bf16[96,3328]{1,0:T(8,128)(2,1)}, bf16[96,3328]{1,0:T(8,128)(2,1)S(1)}, u32[]{:S(2)}, u32[]{:S(2)}) collective-permute-start(bf16[96,3328]{1,0:T(8,128)(2,1)} %collective-permute-done.10.l2), channel_id=1, source_target_pairs={{0,7},{1,0},{2,1},{3,2},{4,3},{5,4},{6,5},{7,6},{8,15},{9,8},{10,9... | collective-permute-start | bytes 1916936 | tf_op jit(solution)/shard_map/ppermute | solution.py:23
  53.9 9.9 %collective-permute-done.4.l2 = bf16[96,3328]{1,0:T(8,128)(2,1)S(1)} collective-permute-done((bf16[96,3328]{1,0:T(8,128)(2,1)S(1)}, bf16[96,3328]{1,0:T(8,128)(2,1)S(1)}, u32[]{:S(2)}, u32[]{:S(2)}) %collective-permute-start.4) | collective-permute-done | bytes 639008 | tf_op jit(solution)/shard_map/ppermute | solution.py:23
  63.8 3.7 %collective-permute-start.5 = (bf16[96,3328]{1,0:T(8,128)(2,1)S(1)}, bf16[96,3328]{1,0:T(8,128)(2,1)S(1)}, u32[]{:S(2)}, u32[]{:S(2)}) collective-permute-start(bf16[96,3328]{1,0:T(8,128)(2,1)S(1)} %collective-permute-done.4.l2), channel_id=1, source_target_pairs={{0,7},{1,0},{2,1},{3,2},{4,3},{5,4},{6,5},{7,6},{8,15},{9,8},{10,9... | collective-permute-start | bytes 1916936 | tf_op jit(solution)/shard_map/ppermute | solution.py:23
  67.5 10.1 %collective-permute-done.11.l3.ref = bf16[96,3328]{1,0:T(8,128)(2,1)S(1)} collective-permute-done((bf16[96,3328]{1,0:T(8,128)(2,1)}, bf16[96,3328]{1,0:T(8,128)(2,1)S(1)}, u32[]{:S(2)}, u32[]{:S(2)}) %collective-permute-start.11) | collective-permute-done | bytes 639008 | tf_op jit(solution)/shard_map/ppermute | solution.py:23
  77.6 3.7 %collective-permute-start.15 = (bf16[48,3328]{1,0:T(8,128)(2,1)S(1)}, bf16[48,3328]{1,0:T(8,128)(2,1)S(1)}, u32[]{:S(2)}, u32[]{:S(2)}) collective-permute-start(bf16[48,3328]{1,0:T(8,128)(2,1)S(1)} %half_of.7), channel_id=1, source_target_pairs={{0,7},{1,0},{2,1},{3,2},{4,3},{5,4},{6,5},{7,6},{8,15},{9,8},{10,9... | collective-permute-start | bytes 958472 | tf_op jit(solution)/shard_map/ppermute | solution.py:23
  81.3 0.3 collective-permute-start.14
  81.6 4.0 %near.2 = (bf16[2,912,1664]{2,1,0:T(8,128)(2,1)S(1)}, f32[2,128,1664]{2,1,0:T(8,128)S(1)}, f32[768,128]{1,0:T(8,128)S(1)}) custom-call(bf16[96,3328]{1,0:T(8,128)(2,1)S(1)} %get-tuple-element.60.own, bf16[96,3328]{1,0:T(8,128)(2,1)} %collective-permute-done.6.r1, bf16[96,3328]{1,0:T(8,128)(2,1)} %collective-permute-done.7.r2, ...), custom_call_target="tpu_custom_call" | custom-call | flops 654311424 | bytes 5111808 | tf_op jit(solution)/shard_map/near/pallas_call | solution.py:117
  85.6 5.6 %collective-permute-done.5.ref.l3 = bf16[96,3328]{1,0:T(8,128)(2,1)S(1)} collective-permute-done((bf16[96,3328]{1,0:T(8,128)(2,1)S(1)}, bf16[96,3328]{1,0:T(8,128)(2,1)S(1)}, u32[]{:S(2)}, u32[]{:S(2)}) %collective-permute-start.5) | collective-permute-done | bytes 639008 | tf_op jit(solution)/shard_map/ppermute | solution.py:23
  91.2 3.7 %collective-permute-done.2.ref.r3 = bf16[96,3328]{1,0:T(8,128)(2,1)S(1)} collective-permute-done((bf16[96,3328]{1,0:T(8,128)(2,1)S(1)}, bf16[96,3328]{1,0:T(8,128)(2,1)S(1)}, u32[]{:S(2)}, u32[]{:S(2)}) %collective-permute-start.2) | collective-permute-done | bytes 639008 | tf_op jit(solution)/shard_map/ppermute | solution.py:23
  94.9 0.0 copy-start
  94.9 0.1 collective-permute-start.13
  95.0 2.0 %collective-permute-start.12 = (bf16[48,3328]{1,0:T(8,128)(2,1)S(1)}, bf16[48,3328]{1,0:T(8,128)(2,1)S(1)}, u32[]{:S(2)}, u32[]{:S(2)}) collective-permute-start(bf16[48,3328]{1,0:T(8,128)(2,1)S(1)} %half_of.4), channel_id=1, source_target_pairs={{0,1},{1,2},{2,3},{3,4},{4,5},{5,6},{6,7},{7,0},{8,9},{9,10},{10,1... | collective-permute-start | bytes 958472 | tf_op jit(solution)/shard_map/ppermute | solution.py:23
  97.0 2.5 %near.3 = (bf16[2,912,1664]{2,1,0:T(8,128)(2,1)S(1)}, f32[2,128,1664]{2,1,0:T(8,128)S(1)}, f32[768,128]{1,0:T(8,128)S(1)}) custom-call(bf16[96,3328]{1,0:T(8,128)(2,1)S(1)} %get-tuple-element.61.own, bf16[96,3328]{1,0:T(8,128)(2,1)S(1)} %collective-permute-done.r1, bf16[96,3328]{1,0:T(8,128)(2,1)S(1)} %collective-permute-done.1.r2, ...), custom_call_target="tpu_custom_call" | custom-call | flops 654311424 | bytes 5111808 | tf_op jit(solution)/shard_map/near/pallas_call | solution.py:117
  99.6 2.2 %collective-permute-done.14.refs_0_ = bf16[48,3328]{1,0:T(8,128)(2,1)S(1)} collective-permute-done((bf16[48,3328]{1,0:T(8,128)(2,1)S(1)}, bf16[48,3328]{1,0:T(8,128)(2,1)S(1)}, u32[]{:S(2)}, u32[]{:S(2)}) %collective-permute-start.14) | collective-permute-done | bytes 319520 | tf_op jit(solution)/shard_map/ppermute | solution.py:23
  101.7 4.6 %far.2 = (bf16[2,912,1664]{2,1,0:T(8,128)(2,1)S(1)}, f32[768,256]{1,0:T(8,128)S(1)}, f32[136,256]{1,0:T(8,128)S(1)}, f32[768,128]{1,0:T(8,128)S(1)}) custom-call(bf16[48,3328]{1,0:T(8,128)(2,1)S(1)} %collective-permute-done.14.refs_0_, bf16[48,3328]{1,0:T(8,128)(2,1)S(1)} %collective-permute-done.15.refs_1_, ...), custom_call_target="tpu_custom_call", output_to_operand_aliasing={{0}: (2, {})} | custom-call | flops 1526726656 | bytes 5111808 | tf_op jit(solution)/shard_map/far/pallas_call | solution.py:204
  106.3 0.9 collective-permute-done.12.refs_0_
  107.1 4.6 %far.3 = (bf16[2,912,1664]{2,1,0:T(8,128)(2,1)S(1)}, f32[768,256]{1,0:T(8,128)S(1)}, f32[136,256]{1,0:T(8,128)S(1)}, f32[768,128]{1,0:T(8,128)S(1)}) custom-call(bf16[48,3328]{1,0:T(8,128)(2,1)S(1)} %collective-permute-done.12.refs_0_, ...), custom_call_target="tpu_custom_call", output_to_operand_aliasing={{0}: (2, {}), {1}: (7, {}), {2}: (8, {}), {3}: (9, {})} | custom-call | flops 1526726656 | bytes 5111808 | tf_op jit(solution)/shard_map/far/pallas_call | solution.py:204
  111.8 0.0 copy-start.1
  111.8 0.2 core_stage.1
  111.9 0.1 collective-permute-start.16
  112.0 1.8 %collective-permute-done.16.refs_1_ = f32[880,128]{1,0:T(8,128)S(1)} collective-permute-done((f32[880,128]{1,0:T(8,128)S(1)}, f32[880,128]{1,0:T(8,128)S(1)}, u32[]{:S(2)}, u32[]{:S(2)}) %collective-permute-start.16) | collective-permute-done | bytes 450592 | tf_op jit(solution)/shard_map/ppermute | solution.py:23
  113.8 0.1 axis_stage.2
  113.9 3.3 %collective-permute-start.17 = (f32[304,128]{1,0:T(8,128)S(1)}, f32[304,128]{1,0:T(8,128)S(1)}, u32[]{:S(2)}, u32[]{:S(2)}) collective-permute-start(f32[304,128]{1,0:T(8,128)S(1)} %get-tuple-element.51), channel_id=1, source_target_pairs={{0,128},{8,40},{16,144},{24,56},{32,160},{40,8},{48,176},{56,24},{... | collective-permute-start | bytes 466952 | tf_op jit(solution)/shard_map/ppermute | solution.py:331
  117.2 0.7 collective-permute-start.18
  117.9 2.6 %collective-permute-start.19 = (f32[304,128]{1,0:T(8,128)S(1)}, f32[304,128]{1,0:T(8,128)S(1)}, u32[]{:S(2)}, u32[]{:S(2)}) collective-permute-start(f32[304,128]{1,0:T(8,128)S(1)} %get-tuple-element.53), channel_id=1, source_target_pairs={{0,192},{8,56},{16,208},{24,8},{32,224},{40,24},{48,240},{56,40},{... | collective-permute-start | bytes 466952 | tf_op jit(solution)/shard_map/ppermute | solution.py:331
  120.4 0.3 collective-permute-done.17.refs_1_
  120.7 2.9 %collective-permute-done.18.refs_2_ = f32[304,128]{1,0:T(8,128)S(1)} collective-permute-done((f32[304,128]{1,0:T(8,128)S(1)}, f32[304,128]{1,0:T(8,128)S(1)}, u32[]{:S(2)}, u32[]{:S(2)}) %collective-permute-start.18) | collective-permute-done | bytes 155680 | tf_op jit(solution)/shard_map/ppermute | solution.py:331
  123.7 1.5 %collective-permute-start.20 = (f32[160,128]{1,0:T(8,128)S(1)}, f32[160,128]{1,0:T(8,128)S(1)}, u32[]{:S(2)}, u32[]{:S(2)}) collective-permute-start(f32[160,128]{1,0:T(8,128)S(1)} %get-tuple-element.55), channel_id=1, source_target_pairs={{0,32},{8,136},{16,48},{24,152},{32,0},{40,168},{48,16},{56,184},{... | collective-permute-start | bytes 245768 | tf_op jit(solution)/shard_map/ppermute | solution.py:331
  125.2 2.1 %collective-permute-start.21 = (f32[160,128]{1,0:T(8,128)S(1)}, f32[160,128]{1,0:T(8,128)S(1)}, u32[]{:S(2)}, u32[]{:S(2)}) collective-permute-start(f32[160,128]{1,0:T(8,128)S(1)} %get-tuple-element.56), channel_id=1, source_target_pairs={{0,16},{8,72},{16,32},{24,88},{32,48},{40,104},{48,0},{56,120},{64... | collective-permute-start | bytes 245768 | tf_op jit(solution)/shard_map/ppermute | solution.py:331
  127.3 2.4 %collective-permute-done.20.refs_1_ = f32[160,128]{1,0:T(8,128)S(1)} collective-permute-done((f32[160,128]{1,0:T(8,128)S(1)}, f32[160,128]{1,0:T(8,128)S(1)}, u32[]{:S(2)}, u32[]{:S(2)}) %collective-permute-start.20) | collective-permute-done | bytes 81952 | tf_op jit(solution)/shard_map/ppermute | solution.py:331
  129.7 3.2 %collective-permute-done.22.refs_3_ = f32[160,128]{1,0:T(8,128)S(1)} collective-permute-done((f32[160,128]{1,0:T(8,128)S(1)}, f32[160,128]{1,0:T(8,128)S(1)}, u32[]{:S(2)}, u32[]{:S(2)}) %collective-permute-start.22) | collective-permute-done | bytes 81952 | tf_op jit(solution)/shard_map/ppermute | solution.py:331
  132.9 3.2 %last_stage.1 = (f32[24,128]{1,0:T(8,128)}, f32[1,128]{1,0:T(1,128)}) custom-call(f32[160,128]{1,0:T(8,128)S(1)} %get-tuple-element.54.refs_0_, f32[160,128]{1,0:T(8,128)S(1)} %collective-permute-done.20.refs_1_, f32[160,128]{1,0:T(8,128)S(1)} %collective-permute-done.21.refs_2_, f32[160,128]{1,0:T(8,128)S(1)} %collective-permute-done.22.refs_3_, ...), custom_call_target="tpu_custom_call" | custom-call | flops 1000000 | bytes 1000000 | tf_op jit(solution)/shard_map/last_stage/pallas_call | solution.py:231
  (20 shorter events, 0.2 us)
Async XLA Ops:
  0.6 10.6 %copy-start.2 = (bf16[24,128]{1,0:T(8,128)(2,1)S(1)}, bf16[24,128]{1,0:T(8,128)(2,1)}, u32[]{:S(2)}) copy-start(bf16[24,128]{1,0:T(8,128)(2,1)} %param.5) | copy-start | bytes 18436
  2.0 20.7 %collective-permute-start.9 = (bf16[96,3328]{1,0:T(8,128)(2,1)S(1)}, bf16[96,3328]{1,0:T(8,128)(2,1)S(1)}, u32[]{:S(2)}, u32[]{:S(2)}) collective-permute-start(bf16[96,3328]{1,0:T(8,128)(2,1)S(1)} %get-tuple-element.60.own), channel_id=1, source_target_pairs={{0,7},{1,0},{2,1},{3,2},{4,3},{5,4},{6,5},{7,6},{8,15},{9,8},{10,9... | collective-permute-start | bytes 1916936 | tf_op jit(solution)/shard_map/ppermute | solution.py:23
  7.9 18.6 %collective-permute-start.6 = (bf16[96,3328]{1,0:T(8,128)(2,1)S(1)}, bf16[96,3328]{1,0:T(8,128)(2,1)}, u32[]{:S(2)}, u32[]{:S(2)}) collective-permute-start(bf16[96,3328]{1,0:T(8,128)(2,1)S(1)} %get-tuple-element.60.own), channel_id=1, source_target_pairs={{0,1},{1,2},{2,3},{3,4},{4,5},{5,6},{6,7},{7,0},{8,9},{9,10},{10,1... | collective-permute-start | bytes 1916936 | tf_op jit(solution)/shard_map/ppermute | solution.py:23
  7.9 32.2 %collective-permute-start = (bf16[96,3328]{1,0:T(8,128)(2,1)S(1)}, bf16[96,3328]{1,0:T(8,128)(2,1)S(1)}, u32[]{:S(2)}, u32[]{:S(2)}) collective-permute-start(bf16[96,3328]{1,0:T(8,128)(2,1)S(1)} %get-tuple-element.61.own), channel_id=1, source_target_pairs={{0,1},{1,2},{2,3},{3,4},{4,5},{5,6},{6,7},{7,0},{8,9},{9,10},{10,1... | collective-permute-start | bytes 1916936 | tf_op jit(solution)/shard_map/ppermute | solution.py:23
  7.9 32.2 %collective-permute-start.3 = (bf16[96,3328]{1,0:T(8,128)(2,1)S(1)}, bf16[96,3328]{1,0:T(8,128)(2,1)S(1)}, u32[]{:S(2)}, u32[]{:S(2)}) collective-permute-start(bf16[96,3328]{1,0:T(8,128)(2,1)S(1)} %get-tuple-element.61.own), channel_id=1, source_target_pairs={{0,7},{1,0},{2,1},{3,2},{4,3},{5,4},{6,5},{7,6},{8,15},{9,8},{10,9... | collective-permute-start | bytes 1916936 | tf_op jit(solution)/shard_map/ppermute | solution.py:23
  11.9 14.6 %all-to-all-start = ((bf16[32,24,128]{2,1,0:T(8,128)(2,1)}), bf16[32,24,128]{2,1,0:T(8,128)(2,1)S(1)}, u32[]{:S(2)}, u32[]{:S(2)}) async-start(bf16[32,24,128]{2,1,0:T(8,128)(2,1)} %broadcast_in_dim.3), calls=%async_computation | async-start | bytes 393216 | tf_op jit(solution)/shard_map/all_to_all | solution.py:29
  22.7 27.4 %collective-permute-start.10 = (bf16[96,3328]{1,0:T(8,128)(2,1)S(1)}, bf16[96,3328]{1,0:T(8,128)(2,1)}, u32[]{:S(2)}, u32[]{:S(2)}) collective-permute-start(bf16[96,3328]{1,0:T(8,128)(2,1)S(1)} %collective-permute-done.9.l1), channel_id=1, source_target_pairs={{0,7},{1,0},{2,1},{3,2},{4,3},{5,4},{6,5},{7,6},{8,15},{9,8},{10,9... | collective-permute-start | bytes 1916936 | tf_op jit(solution)/shard_map/ppermute | solution.py:23
  26.5 27.4 %collective-permute-start.7 = (bf16[96,3328]{1,0:T(8,128)(2,1)}, bf16[96,3328]{1,0:T(8,128)(2,1)}, u32[]{:S(2)}, u32[]{:S(2)}) collective-permute-start(bf16[96,3328]{1,0:T(8,128)(2,1)} %collective-permute-done.6.r1), channel_id=1, source_target_pairs={{0,1},{1,2},{2,3},{3,4},{4,5},{5,6},{6,7},{7,0},{8,9},{9,10},{10,1... | collective-permute-start | bytes 1916936 | tf_op jit(solution)/shard_map/ppermute | solution.py:23
  40.1 23.7 %collective-permute-start.4 = (bf16[96,3328]{1,0:T(8,128)(2,1)S(1)}, bf16[96,3328]{1,0:T(8,128)(2,1)S(1)}, u32[]{:S(2)}, u32[]{:S(2)}) collective-permute-start(bf16[96,3328]{1,0:T(8,128)(2,1)S(1)} %collective-permute-done.3.l1), channel_id=1, source_target_pairs={{0,7},{1,0},{2,1},{3,2},{4,3},{5,4},{6,5},{7,6},{8,15},{9,8},{10,9... | collective-permute-start | bytes 1916936 | tf_op jit(solution)/shard_map/ppermute | solution.py:23
  40.1 27.4 %collective-permute-start.1 = (bf16[96,3328]{1,0:T(8,128)(2,1)S(1)}, bf16[96,3328]{1,0:T(8,128)(2,1)S(1)}, u32[]{:S(2)}, u32[]{:S(2)}) collective-permute-start(bf16[96,3328]{1,0:T(8,128)(2,1)S(1)} %collective-permute-done.r1), channel_id=1, source_target_pairs={{0,1},{1,2},{2,3},{3,4},{4,5},{5,6},{6,7},{7,0},{8,9},{9,10},{10,1... | collective-permute-start | bytes 1916936 | tf_op jit(solution)/shard_map/ppermute | solution.py:23
  50.1 27.5 %collective-permute-start.11 = (bf16[96,3328]{1,0:T(8,128)(2,1)}, bf16[96,3328]{1,0:T(8,128)(2,1)S(1)}, u32[]{:S(2)}, u32[]{:S(2)}) collective-permute-start(bf16[96,3328]{1,0:T(8,128)(2,1)} %collective-permute-done.10.l2), channel_id=1, source_target_pairs={{0,7},{1,0},{2,1},{3,2},{4,3},{5,4},{6,5},{7,6},{8,15},{9,8},{10,9... | collective-permute-start | bytes 1916936 | tf_op jit(solution)/shard_map/ppermute | solution.py:23
  53.9 27.4 %collective-permute-start.8 = (bf16[96,3328]{1,0:T(8,128)(2,1)}, bf16[96,3328]{1,0:T(8,128)(2,1)S(1)}, u32[]{:S(2)}, u32[]{:S(2)}) collective-permute-start(bf16[96,3328]{1,0:T(8,128)(2,1)} %collective-permute-done.7.r2), channel_id=1, source_target_pairs={{0,1},{1,2},{2,3},{3,4},{4,5},{5,6},{6,7},{7,0},{8,9},{9,10},{10,1... | collective-permute-start | bytes 1916936 | tf_op jit(solution)/shard_map/ppermute | solution.py:23
  63.8 27.4 %collective-permute-start.5 = (bf16[96,3328]{1,0:T(8,128)(2,1)S(1)}, bf16[96,3328]{1,0:T(8,128)(2,1)S(1)}, u32[]{:S(2)}, u32[]{:S(2)}) collective-permute-start(bf16[96,3328]{1,0:T(8,128)(2,1)S(1)} %collective-permute-done.4.l2), channel_id=1, source_target_pairs={{0,7},{1,0},{2,1},{3,2},{4,3},{5,4},{6,5},{7,6},{8,15},{9,8},{10,9... | collective-permute-start | bytes 1916936 | tf_op jit(solution)/shard_map/ppermute | solution.py:23
  67.5 27.4 %collective-permute-start.2 = (bf16[96,3328]{1,0:T(8,128)(2,1)S(1)}, bf16[96,3328]{1,0:T(8,128)(2,1)S(1)}, u32[]{:S(2)}, u32[]{:S(2)}) collective-permute-start(bf16[96,3328]{1,0:T(8,128)(2,1)S(1)} %collective-permute-done.1.r2), channel_id=1, source_target_pairs={{0,1},{1,2},{2,3},{3,4},{4,5},{5,6},{6,7},{7,0},{8,9},{9,10},{10,1... | collective-permute-start | bytes 1916936 | tf_op jit(solution)/shard_map/ppermute | solution.py:23
  77.6 21.9 %collective-permute-start.15 = (bf16[48,3328]{1,0:T(8,128)(2,1)S(1)}, bf16[48,3328]{1,0:T(8,128)(2,1)S(1)}, u32[]{:S(2)}, u32[]{:S(2)}) collective-permute-start(bf16[48,3328]{1,0:T(8,128)(2,1)S(1)} %half_of.7), channel_id=1, source_target_pairs={{0,7},{1,0},{2,1},{3,2},{4,3},{5,4},{6,5},{7,6},{8,15},{9,8},{10,9... | collective-permute-start | bytes 958472 | tf_op jit(solution)/shard_map/ppermute | solution.py:23
  81.3 20.4 %collective-permute-start.14 = (bf16[48,3328]{1,0:T(8,128)(2,1)S(1)}, bf16[48,3328]{1,0:T(8,128)(2,1)S(1)}, u32[]{:S(2)}, u32[]{:S(2)}) collective-permute-start(bf16[48,3328]{1,0:T(8,128)(2,1)S(1)} %half_of.6), channel_id=1, source_target_pairs={{0,1},{1,2},{2,3},{3,4},{4,5},{5,6},{6,7},{7,0},{8,9},{9,10},{10,1... | collective-permute-start | bytes 958472 | tf_op jit(solution)/shard_map/ppermute | solution.py:23
  94.9 6.8 %copy-start = (bf16[6656,128]{1,0:T(8,128)(2,1)S(1)}, bf16[6656,128]{1,0:T(8,128)(2,1)}, u32[]{:S(2)}) copy-start(bf16[6656,128]{1,0:T(8,128)(2,1)} %refs_5_.3) | copy-start | bytes 5111812
  94.9 11.3 %collective-permute-start.13 = (bf16[48,3328]{1,0:T(8,128)(2,1)S(1)}, bf16[48,3328]{1,0:T(8,128)(2,1)S(1)}, u32[]{:S(2)}, u32[]{:S(2)}) collective-permute-start(bf16[48,3328]{1,0:T(8,128)(2,1)S(1)} %half_of.5), channel_id=1, source_target_pairs={{0,7},{1,0},{2,1},{3,2},{4,3},{5,4},{6,5},{7,6},{8,15},{9,8},{10,9... | collective-permute-start | bytes 958472 | tf_op jit(solution)/shard_map/ppermute | solution.py:23
  95.0 12.1 %collective-permute-start.12 = (bf16[48,3328]{1,0:T(8,128)(2,1)S(1)}, bf16[48,3328]{1,0:T(8,128)(2,1)S(1)}, u32[]{:S(2)}, u32[]{:S(2)}) collective-permute-start(bf16[48,3328]{1,0:T(8,128)(2,1)S(1)} %half_of.4), channel_id=1, source_target_pairs={{0,1},{1,2},{2,3},{3,4},{4,5},{5,6},{6,7},{7,0},{8,9},{9,10},{10,1... | collective-permute-start | bytes 958472 | tf_op jit(solution)/shard_map/ppermute | solution.py:23
  111.8 21.2 %copy-start.1 = (f32[1024]{0:T(1024)S(1)}, f32[1024]{0:T(1024)}, u32[]{:S(2)}) copy-start(f32[1024]{0:T(1024)} %param.6) | copy-start | bytes 12292
  111.9 1.9 %collective-permute-start.16 = (f32[880,128]{1,0:T(8,128)S(1)}, f32[880,128]{1,0:T(8,128)S(1)}, u32[]{:S(2)}, u32[]{:S(2)}) collective-permute-start(f32[880,128]{1,0:T(8,128)S(1)} %get-tuple-element.49), channel_id=1, source_target_pairs={{0,8},{8,0},{1,9},{9,1},{2,10},{10,2},{3,11},{11,3},{4,12},{12,4},... | collective-permute-start | bytes 1351688 | tf_op jit(solution)/shard_map/ppermute | solution.py:23
  113.9 6.8 %collective-permute-start.17 = (f32[304,128]{1,0:T(8,128)S(1)}, f32[304,128]{1,0:T(8,128)S(1)}, u32[]{:S(2)}, u32[]{:S(2)}) collective-permute-start(f32[304,128]{1,0:T(8,128)S(1)} %get-tuple-element.51), channel_id=1, source_target_pairs={{0,128},{8,40},{16,144},{24,56},{32,160},{40,8},{48,176},{56,24},{... | collective-permute-start | bytes 466952 | tf_op jit(solution)/shard_map/ppermute | solution.py:331
  117.2 6.4 %collective-permute-start.18 = (f32[304,128]{1,0:T(8,128)S(1)}, f32[304,128]{1,0:T(8,128)S(1)}, u32[]{:S(2)}, u32[]{:S(2)}) collective-permute-start(f32[304,128]{1,0:T(8,128)S(1)} %get-tuple-element.52), channel_id=1, source_target_pairs={{0,64},{8,24},{16,80},{24,40},{32,96},{40,56},{48,112},{56,8},{64,... | collective-permute-start | bytes 466952 | tf_op jit(solution)/shard_map/ppermute | solution.py:331
  117.9 5.8 %collective-permute-start.19 = (f32[304,128]{1,0:T(8,128)S(1)}, f32[304,128]{1,0:T(8,128)S(1)}, u32[]{:S(2)}, u32[]{:S(2)}) collective-permute-start(f32[304,128]{1,0:T(8,128)S(1)} %get-tuple-element.53), channel_id=1, source_target_pairs={{0,192},{8,56},{16,208},{24,8},{32,224},{40,24},{48,240},{56,40},{... | collective-permute-start | bytes 466952 | tf_op jit(solution)/shard_map/ppermute | solution.py:331
  123.7 6.0 %collective-permute-start.20 = (f32[160,128]{1,0:T(8,128)S(1)}, f32[160,128]{1,0:T(8,128)S(1)}, u32[]{:S(2)}, u32[]{:S(2)}) collective-permute-start(f32[160,128]{1,0:T(8,128)S(1)} %get-tuple-element.55), channel_id=1, source_target_pairs={{0,32},{8,136},{16,48},{24,152},{32,0},{40,168},{48,16},{56,184},{... | collective-permute-start | bytes 245768 | tf_op jit(solution)/shard_map/ppermute | solution.py:331
  125.2 4.5 %collective-permute-start.21 = (f32[160,128]{1,0:T(8,128)S(1)}, f32[160,128]{1,0:T(8,128)S(1)}, u32[]{:S(2)}, u32[]{:S(2)}) collective-permute-start(f32[160,128]{1,0:T(8,128)S(1)} %get-tuple-element.56), channel_id=1, source_target_pairs={{0,16},{8,72},{16,32},{24,88},{32,48},{40,104},{48,0},{56,120},{64... | collective-permute-start | bytes 245768 | tf_op jit(solution)/shard_map/ppermute | solution.py:331
  127.3 5.7 %collective-permute-start.22 = (f32[160,128]{1,0:T(8,128)S(1)}, f32[160,128]{1,0:T(8,128)S(1)}, u32[]{:S(2)}, u32[]{:S(2)}) collective-permute-start(f32[160,128]{1,0:T(8,128)S(1)} %get-tuple-element.57), channel_id=1, source_target_pairs={{0,48},{8,200},{16,0},{24,216},{32,16},{40,232},{48,32},{56,248},{... | collective-permute-start | bytes 245768 | tf_op jit(solution)/shard_map/ppermute | solution.py:331
